TPU v7x, 32 devices: a whole 2x2x4 slice. The times are simulated.
32 devices in a mesh: gx: 8 (over z, core), gy: 4 (over y, x).
Axes of the slice: x: 2, y: 2, z: 4, core: 2. Of those that a mesh axis runs over, the one named last changes fastest.
Arguments:
- potential: float32 [32, 64, 256], P('gx', 'gy'), may hold values from -0.2 to 1.2
- recovery: float32 [32, 64, 256], P('gx', 'gy'), may hold values from 0 to 1.5
- fiber_angles: float32 [2, 32, 64, 256], P(None, 'gx', 'gy'), may hold values from -3.140625 to 3.140625
- deform: float32 [9, 8192], P(None, ('gx', 'gy')), may hold values from -0.15 to 1.25, as said below
- elem_slot: int32 [8, 16, 64], P('gx', 'gy'), may hold values from 0 to 8191, as said below
Outputs:
- potential_next: float32 [32, 64, 256], P('gx', 'gy')
- recovery_next: float32 [32, 64, 256], P('gx', 'gy')
Inputs may be any that keep to these rules, and one draw needn't show every extreme that they name: `elem_slot`: entries are distinct. Slot s lies on device s / 256 (rounded down) of gx+gy. The elements of one device's block along gx and gy lie in the slots of the devices with the same index along gx, exactly 64 of them in each. `deform`: components 0, 4 and 8 (the diagonal of F) lie in 0.8 to 1.25, the other six in -0.15 to 0.15.
All inputs are finite; a program needn't handle non-finite values.
Results may differ from a plain program's by a relative error of at most 0.0003.
Values sent between devices are 32-bit elements; how exact they have to be, the bound alone decides.
No kernel may reach another device: no remote copies, remote signals or barrier semaphores. Data moves between devices by JAX's collectives and lax.ppermute only.
A program may use at most 64 MiB of HBM per device.

v0:
```python
import jax
import jax.numpy as jnp
from jax import lax
from jax.sharding import PartitionSpec as P

RATIO = 4


sigma_fiber = 1.0
sigma_cross = 0.3
time_step = 0.1
excite_gain = 8.0
excite_level = 0.15
stretch_gain = 10.0
stretch_reversal = 0.6
recover_rate = 0.5


def padded_2(block, sides, width):
    for axis, dim in sides:
        count = lax.axis_size(axis)
        forward = [(i, i + 1) for i in range(count - 1)]
        backward = [(target, source) for source, target in forward]
        low = lax.ppermute(
            lax.slice_in_dim(block, block.shape[dim] - width, None, axis=dim), axis, forward
        )
        high = lax.ppermute(lax.slice_in_dim(block, 0, width, axis=dim), axis, backward)
        block = jnp.concatenate([low, block, high], axis=dim)
    return block


def refine(padded, dim):
    inner_size = padded.shape[dim] - 2
    lower = lax.slice_in_dim(padded, 0, inner_size, axis=dim)
    middle = lax.slice_in_dim(padded, 1, inner_size + 1, axis=dim)
    upper = lax.slice_in_dim(padded, 2, inner_size + 2, axis=dim)
    pieces = []
    for position in range(RATIO):
        offset = (position + 0.5) / RATIO - 0.5
        weight = abs(offset)
        neighbor = lower if offset < 0 else upper
        pieces.append((1.0 - weight) * middle + weight * neighbor)
    stacked = jnp.stack(pieces, axis=dim + 1)
    new_shape = list(padded.shape)
    new_shape[dim] = inner_size * RATIO
    return stacked.reshape(new_shape)


def refine_wide(padded, dim):
    weight = 0.5 - 0.5 / RATIO
    extent = padded.shape[dim]
    low_rim = (1.0 - weight) * lax.slice_in_dim(padded, 0, 1, axis=dim) + weight * lax.slice_in_dim(
        padded, 1, 2, axis=dim
    )
    high_rim = (1.0 - weight) * lax.slice_in_dim(
        padded, extent - 1, extent, axis=dim
    ) + weight * lax.slice_in_dim(padded, extent - 2, extent - 1, axis=dim)
    return jnp.concatenate([low_rim, refine(padded, dim), high_rim], axis=dim)


def directions(angles):
    azimuth = angles[0]
    elevation = angles[1]
    return jnp.stack(
        [
            jnp.cos(azimuth) * jnp.cos(elevation),
            jnp.sin(azimuth) * jnp.cos(elevation),
            jnp.sin(elevation),
        ]
    )


def tensors(field, fiber):
    entries = [field[number] for number in range(9)]

    def element(row_index, col_index):
        return entries[3 * (row_index % 3) + col_index % 3]

    cofactor = [
        [
            element(row_index + 1, col_index + 1) * element(row_index + 2, col_index + 2)
            - element(row_index + 1, col_index + 2) * element(row_index + 2, col_index + 1)
            for col_index in range(3)
        ]
        for row_index in range(3)
    ]
    determinant = (
        element(0, 0) * cofactor[0][0]
        + element(0, 1) * cofactor[0][1]
        + element(0, 2) * cofactor[0][2]
    )
    inverse = [
        [cofactor[col_index][row_index] / determinant for col_index in range(3)]
        for row_index in range(3)
    ]
    stretched = [
        element(row_index, 0) * fiber[0]
        + element(row_index, 1) * fiber[1]
        + element(row_index, 2) * fiber[2]
        for row_index in range(3)
    ]
    stretch = jnp.sqrt(
        stretched[0] * stretched[0] + stretched[1] * stretched[1] + stretched[2] * stretched[2]
    )
    pulled = [
        inverse[row_index][0] * fiber[0]
        + inverse[row_index][1] * fiber[1]
        + inverse[row_index][2] * fiber[2]
        for row_index in range(3)
    ]
    conduct = []
    for first_index, second_index in ((0, 0), (1, 1), (2, 2), (0, 1), (0, 2), (1, 2)):
        metric = (
            inverse[first_index][0] * inverse[second_index][0]
            + inverse[first_index][1] * inverse[second_index][1]
            + inverse[first_index][2] * inverse[second_index][2]
        )
        conduct.append(
            sigma_cross * metric
            + (sigma_fiber - sigma_cross) * pulled[first_index] * pulled[second_index]
        )
    return (jnp.stack(conduct), stretch)


def close_faces(flux, dim, at_first, at_last):
    extent = flux.shape[dim]
    face_index = lax.broadcasted_iota(jnp.int32, flux.shape, dim)
    closed = (face_index == 0) & at_first | (face_index == extent - 1) & at_last
    return jnp.where(closed, jnp.zeros_like(flux), flux)


def divergence(potential_pad, tensor_pad, first_x, last_x, first_y, last_y):
    grad_x = (potential_pad[2:, :, :] - potential_pad[:-2, :, :]) * 0.5
    grad_y = (potential_pad[:, 2:, :] - potential_pad[:, :-2, :]) * 0.5
    grad_z = (potential_pad[:, :, 2:] - potential_pad[:, :, :-2]) * 0.5

    def face_mean(component, dim):
        inner = tensor_pad[component]
        if dim == 0:
            inner = inner[:, 1:-1, 1:-1]
        elif dim == 1:
            inner = inner[1:-1, :, 1:-1]
        else:
            inner = inner[1:-1, 1:-1, :]
        extent = inner.shape[dim]
        return (
            lax.slice_in_dim(inner, 1, extent, axis=dim)
            + lax.slice_in_dim(inner, 0, extent - 1, axis=dim)
        ) * 0.5

    step_x = potential_pad[1:, 1:-1, 1:-1] - potential_pad[:-1, 1:-1, 1:-1]
    mean_y = (grad_y[1:, :, 1:-1] + grad_y[:-1, :, 1:-1]) * 0.5
    mean_z = (grad_z[1:, 1:-1, :] + grad_z[:-1, 1:-1, :]) * 0.5
    flux_x = face_mean(0, 0) * step_x + face_mean(3, 0) * mean_y + face_mean(4, 0) * mean_z
    flux_x = close_faces(flux_x, 0, first_x, last_x)
    step_y = potential_pad[1:-1, 1:, 1:-1] - potential_pad[1:-1, :-1, 1:-1]
    mean_x = (grad_x[:, 1:, 1:-1] + grad_x[:, :-1, 1:-1]) * 0.5
    mean_z = (grad_z[1:-1, 1:, :] + grad_z[1:-1, :-1, :]) * 0.5
    flux_y = face_mean(3, 1) * mean_x + face_mean(1, 1) * step_y + face_mean(5, 1) * mean_z
    flux_y = close_faces(flux_y, 1, first_y, last_y)
    step_z = potential_pad[1:-1, 1:-1, 1:] - potential_pad[1:-1, 1:-1, :-1]
    mean_x = (grad_x[:, 1:-1, 1:] + grad_x[:, 1:-1, :-1]) * 0.5
    mean_y = (grad_y[1:-1, :, 1:] + grad_y[1:-1, :, :-1]) * 0.5
    flux_z = face_mean(4, 2) * mean_x + face_mean(5, 2) * mean_y + face_mean(2, 2) * step_z
    flux_z = close_faces(flux_z, 2, True, True)
    return (
        flux_x[1:]
        - flux_x[:-1]
        + (flux_y[:, 1:] - flux_y[:, :-1])
        + (flux_z[:, :, 1:] - flux_z[:, :, :-1])
    )


def update(voltage, recovery, divergent, stretch):
    current = (
        excite_gain * voltage * (voltage - excite_level) * (voltage - 1.0) + voltage * recovery
    )
    current = current + stretch_gain * jnp.maximum(stretch - 1.0, 0.0) * (
        voltage - stretch_reversal
    )
    voltage_next = voltage + time_step * (divergent - current)
    recovery_next = recovery + time_step * recover_rate * (
        -recovery - excite_gain * voltage * (voltage - excite_level - 1.0)
    )
    return (voltage_next, recovery_next)


def clamp_rim(extended, dim, at_first, at_last):
    extent = extended.shape[dim]
    low_rim = jnp.where(
        at_first,
        lax.slice_in_dim(extended, 1, 2, axis=dim),
        lax.slice_in_dim(extended, 0, 1, axis=dim),
    )
    high_rim = jnp.where(
        at_last,
        lax.slice_in_dim(extended, extent - 2, extent - 1, axis=dim),
        lax.slice_in_dim(extended, extent - 1, extent, axis=dim),
    )
    return jnp.concatenate(
        [low_rim, lax.slice_in_dim(extended, 1, extent - 1, axis=dim), high_rim], axis=dim
    )


def pad_last(values):
    widths = [(0, 0)] * (values.ndim - 1) + [(1, 1)]
    return jnp.pad(values, widths, mode="edge")


def local(potential, recovery, fiber_angles, deform, elem_slot):
    block_x, block_y, block_z = elem_slot.shape
    components = deform.shape[0]
    held_count = deform.shape[1]
    across = lax.axis_size("gx")
    down_count = lax.axis_size("gy")
    at_first_x = lax.axis_index("gx") == 0
    at_last_x = lax.axis_index("gx") == across - 1
    at_first_y = lax.axis_index("gy") == 0
    at_last_y = lax.axis_index("gy") == down_count - 1
    flat_slots = elem_slot.reshape(-1)
    sort_order = jnp.argsort(flat_slots)
    wanted = (flat_slots[sort_order] % held_count).reshape(down_count, -1)
    asked_slots = lax.all_to_all(wanted, "gy", split_axis=0, concat_axis=0, tiled=True)
    picked = deform[:, asked_slots.reshape(-1)].reshape(components, down_count, -1)
    answered = lax.all_to_all(picked, "gy", split_axis=1, concat_axis=1, tiled=True)
    coarse = jnp.zeros((components, flat_slots.shape[0]), jnp.float32)
    coarse = coarse.at[:, sort_order].set(answered.reshape(components, -1))
    coarse = coarse.reshape(components, block_x, block_y, block_z)
    coarse = padded_2(coarse, (("gx", 1), ("gy", 2)), 1)
    coarse = pad_last(
        clamp_rim(clamp_rim(coarse, 1, at_first_x, at_last_x), 2, at_first_y, at_last_y)
    )
    fine_field = refine(refine_wide(refine_wide(coarse, 1), 2), 3)
    angles_wide = padded_2(fiber_angles, (("gx", 1), ("gy", 2)), 1)
    conduct, stretch = tensors(fine_field, directions(angles_wide))
    stretch = stretch[1:-1, 1:-1]
    tensor_pad = pad_last(conduct)
    neighbors = padded_2(potential, (("gx", 0), ("gy", 1)), 1)
    potential_pad = pad_last(
        clamp_rim(clamp_rim(neighbors, 0, at_first_x, at_last_x), 1, at_first_y, at_last_y)
    )
    divergent = divergence(potential_pad, tensor_pad, at_first_x, at_last_x, at_first_y, at_last_y)
    return update(potential, recovery, divergent, stretch)


def solution(mesh):
    placed = (
        P("gx", "gy", None),
        P("gx", "gy", None),
        P(None, "gx", "gy", None),
        P(None, ("gx", "gy")),
        P("gx", "gy", None),
    )
    return jax.shard_map(
        local,
        mesh=mesh,
        in_specs=placed,
        out_specs=(P("gx", "gy", None), P("gx", "gy", None)),
        check_vma=False,
    )
```

profile of v0, /device:TPU:0, one launch (start us, length us, event | category | flops | bytes accessed | tf_op | source)
XLA Modules:
  0.0 99.9 jit_solution(9463944152631830109)
XLA Ops:
  0.6 0.8 reshape.1500
  1.4 3.2 %sort.17 = (s32[256]{0:T(256)}, s32[256]{0:T(256)S(1)}) sort(s32[256]{0:T(256)S(1)} %reshape.1500, s32[256]{0:T(256)S(1)} %iota.29), dimensions={0}, to_apply=%region_0.0 | sort | flops 2048 | bytes 4096 | tf_op jit(solution)/shard_map/jit(argsort)/sort | solution.py:221
  4.6 1.9 %gather_fusion = s32[256]{0:T(256)S(1)} fusion(s32[256]{0:T(256)S(1)} %reshape.1500, s32[1024]{0:T(1024)S(1)} %pad_clamp_fusion.1), kind=kCustom, calls=%fused_computation | custom fusion | bytes 3072 | tf_op jit(solution)/shard_map/gather | solution.py:222
  6.6 0.6 and_select_fusion
  7.2 5.2 %all-to-all-start = ((s32[4,1,64]{2,1,0:T(1,128)}), s32[4,1,64]{2,1,0:T(1,128)S(1)}, u32[]{:S(2)}, u32[]{:S(2)}) async-start(s32[4,1,64]{2,1,0:T(1,128)} %and_select_fusion), calls=%async_computation | async-start | bytes 4096 | tf_op jit(solution)/shard_map/all_to_all | solution.py:223
  12.4 0.7 fusion.88
  13.1 1.3 %collective-permute-start.9 = (f32[1,16,256]{2,1,0:T(8,128)S(1)}, f32[1,16,256]{2,1,0:T(8,128)S(1)}, u32[]{:S(2)}, u32[]{:S(2)}) collective-permute-start(f32[1,16,256]{2,1,0:T(8,128)S(1)} %get-tuple-element.89), channel_id=1, source_target_pairs={{4,0},{8,4},{12,8},{16,12},{20,16},{24,20},{28,24},{5,1},{9,5},{13... | collective-permute-start | bytes 49160 | tf_op jit(solution)/shard_map/ppermute | solution.py:27
  14.4 3.0 %collective-permute-start.8 = (f32[1,16,256]{2,1,0:T(8,128)S(1)}, f32[1,16,256]{2,1,0:T(8,128)S(1)}, u32[]{:S(2)}, u32[]{:S(2)}) collective-permute-start(f32[1,16,256]{2,1,0:T(8,128)S(1)} %get-tuple-element.90), channel_id=1, source_target_pairs={{0,4},{4,8},{8,12},{12,16},{16,20},{20,24},{24,28},{1,5},{5,9},{9,... | collective-permute-start | bytes 49160 | tf_op jit(solution)/shard_map/ppermute | solution.py:24
  17.5 0.8 fusion.85
  18.2 1.3 %collective-permute-start.5 = (f32[2,1,16,256]{3,2,1,0:T(8,128)S(1)}, f32[2,1,16,256]{3,2,1,0:T(8,128)S(1)}, u32[]{:S(2)}, u32[]{:S(2)}) collective-permute-start(f32[2,1,16,256]{3,2,1,0:T(8,128)S(1)} %get-tuple-element.66), channel_id=1, source_target_pairs={{4,0},{8,4},{12,8},{16,12},{20,16},{24,20},{28,24},{5,1},{9,5},{13... | collective-permute-start | bytes 98312 | tf_op jit(solution)/shard_map/ppermute | solution.py:27
  19.5 3.7 %collective-permute-start.4 = (f32[2,1,16,256]{3,2,1,0:T(8,128)S(1)}, f32[2,1,16,256]{3,2,1,0:T(8,128)S(1)}, u32[]{:S(2)}, u32[]{:S(2)}) collective-permute-start(f32[2,1,16,256]{3,2,1,0:T(8,128)S(1)} %get-tuple-element.67), channel_id=1, source_target_pairs={{0,4},{4,8},{8,12},{12,16},{16,20},{20,24},{24,28},{1,5},{5,9},{9,... | collective-permute-start | bytes 98312 | tf_op jit(solution)/shard_map/ppermute | solution.py:24
  23.3 0.5 fusion.80
  23.8 0.6 and_or_fusion
  24.4 0.8 copy.319
  25.2 0.5 broadcast.309
  25.7 0.7 reduce.3
  26.5 0.7 gather_fusion.1
  27.3 0.7 reshape.1544
  28.0 4.2 %all-to-all-start.1 = ((f32[4,1,576]{2,1,0:T(1,128)}), f32[4,1,576]{2,1,0:T(1,128)S(1)}, u32[]{:S(2)}, u32[]{:S(2)}) async-start(f32[4,1,576]{2,1,0:T(1,128)} %reshape.1544), calls=%async_computation.1 | async-start | bytes 20480 | tf_op jit(solution)/shard_map/all_to_all | solution.py:225
  32.2 0.5 and_or_fusion.1
  32.7 4.2 %all-to-all-done.1 = f32[4,1,576]{2,1,0:T(1,128)S(1)} async-done(((f32[4,1,576]{2,1,0:T(1,128)}), f32[4,1,576]{2,1,0:T(1,128)S(1)}, u32[]{:S(2)}, u32[]{:S(2)}) %all-to-all-start.1) | async-done | bytes 9248 | tf_op jit(solution)/shard_map/all_to_all | solution.py:225
  36.9 0.5 broadcast.310
  37.4 0.7 reduce.4
  38.4 1.2 %scatter_custom_fusion = f32[9,256]{0,1:T(8,128)S(1)} fusion(s32[256]{0:T(256)S(1)} %compare_select_fusion.3, f32[256,9]{1,0:T(8,128)S(1)} %copy.322, f32[]{:T(128)} %constant.31.clone.1), kind=kCustom, calls=%fused_computation.163 | custom fusion | bytes 9220 | tf_op jit(solution)/shard_map/scatter | solution.py:227
  39.7 1.3 %collective-permute-start.1 = (f32[9,1,4,64]{3,2,0,1:T(4,128)S(1)}, f32[9,1,4,64]{3,2,0,1:T(4,128)S(1)}, u32[]{:S(2)}, u32[]{:S(2)}) collective-permute-start(f32[9,1,4,64]{3,2,0,1:T(4,128)S(1)} %copy.323), channel_id=1, source_target_pairs={{4,0},{8,4},{12,8},{16,12},{20,16},{24,20},{28,24},{5,1},{9,5},{13... | collective-permute-start | bytes 27656 | tf_op jit(solution)/shard_map/ppermute | solution.py:27
  41.0 3.0 %collective-permute-start = (f32[9,1,4,64]{3,2,0,1:T(4,128)S(1)}, f32[9,1,4,64]{3,2,0,1:T(4,128)S(1)}, u32[]{:S(2)}, u32[]{:S(2)}) collective-permute-start(f32[9,1,4,64]{3,2,0,1:T(4,128)S(1)} %copy.323), channel_id=1, source_target_pairs={{0,4},{4,8},{8,12},{12,16},{16,20},{20,24},{24,28},{1,5},{5,9},{9,... | collective-permute-start | bytes 27656 | tf_op jit(solution)/shard_map/ppermute | solution.py:24
  44.0 1.5 %multiply_add_fusion.4 = (f32[4,16,256]{2,1,0:T(8,128)}, f32[6,16,256]{2,1,0:T(8,128)S(1)}) fusion(f32[4,16,256]{2,1,0:T(8,128)} %param.6, f32[4,16,256]{2,1,0:T(8,128)} %param.5, f32[6,16,256]{2,1,0:T(8,128)S(1)} %constant_dynamic-update-slice_fusion.5), kind=kLoop, calls=%fused_computation.162 | loop fusion | flops 114688 | bytes 262144 | tf_op jit(solution)/shard_map/add | solution.py:182
  45.6 2.5 %collective-permute-start.10 = (f32[6,1,256]{2,1,0:T(1,128)S(1)}, f32[6,1,256]{2,1,0:T(1,128)S(1)}, u32[]{:S(2)}, u32[]{:S(2)}) collective-permute-start(f32[6,1,256]{2,1,0:T(1,128)S(1)} %get-tuple-element.85), channel_id=1, source_target_pairs={{0,1},{1,2},{2,3},{4,5},{5,6},{6,7},{8,9},{9,10},{10,11},{12,13},{... | collective-permute-start | bytes 18440 | tf_op jit(solution)/shard_map/ppermute | solution.py:24
  48.1 1.3 %collective-permute-start.11 = (f32[6,1,256]{2,1,0:T(1,128)S(1)}, f32[6,1,256]{2,1,0:T(1,128)S(1)}, u32[]{:S(2)}, u32[]{:S(2)}) collective-permute-start(f32[6,1,256]{2,1,0:T(1,128)S(1)} %get-tuple-element.86), channel_id=1, source_target_pairs={{1,0},{2,1},{3,2},{5,4},{6,5},{7,6},{9,8},{10,9},{11,10},{13,12},{... | collective-permute-start | bytes 18440 | tf_op jit(solution)/shard_map/ppermute | solution.py:27
  49.4 4.5 %collective-permute-start.2 = (f32[9,3,1,64]{3,2,0,1:T(1,128)S(1)}, f32[9,3,1,64]{3,2,0,1:T(1,128)S(1)}, u32[]{:S(2)}, u32[]{:S(2)}) collective-permute-start(f32[9,3,1,64]{3,2,0,1:T(1,128)S(1)} %get-tuple-element.91), channel_id=1, source_target_pairs={{0,1},{1,2},{2,3},{4,5},{5,6},{6,7},{8,9},{9,10},{10,11},{12,13},{... | collective-permute-start | bytes 20744 | tf_op jit(solution)/shard_map/ppermute | solution.py:24
  54.0 1.3 %collective-permute-start.3 = (f32[9,3,1,64]{3,2,0,1:T(1,128)S(1)}, f32[9,3,1,64]{3,2,0,1:T(1,128)S(1)}, u32[]{:S(2)}, u32[]{:S(2)}) collective-permute-start(f32[9,3,1,64]{3,2,0,1:T(1,128)S(1)} %get-tuple-element.92), channel_id=1, source_target_pairs={{1,0},{2,1},{3,2},{5,4},{6,5},{7,6},{9,8},{10,9},{11,10},{13,12},{... | collective-permute-start | bytes 20744 | tf_op jit(solution)/shard_map/ppermute | solution.py:27
  56.1 4.0 %collective-permute-done.3 = f32[9,3,1,64]{3,2,0,1:T(1,128)S(1)} collective-permute-done((f32[9,3,1,64]{3,2,0,1:T(1,128)S(1)}, f32[9,3,1,64]{3,2,0,1:T(1,128)S(1)}, u32[]{:S(2)}, u32[]{:S(2)}) %collective-permute-start.3) | collective-permute-done | bytes 6944 | tf_op jit(solution)/shard_map/ppermute | solution.py:27
  61.3 0.4 add_bitcast_fusion.3
  62.0 0.7 copy-done.5
  62.7 0.6 copy.407
  63.4 0.6 copy.408
  64.0 1.3 %collective-permute-start.7 = (f32[2,6,1,256]{3,0,2,1:T(2,128)}, f32[2,6,1,256]{3,0,2,1:T(2,128)}, u32[]{:S(2)}, u32[]{:S(2)}) collective-permute-start(f32[2,6,1,256]{3,0,2,1:T(2,128)} %copy.408), channel_id=1, source_target_pairs={{1,0},{2,1},{3,2},{5,4},{6,5},{7,6},{9,8},{10,9},{11,10},{13,12},{... | collective-permute-start | bytes 36872 | tf_op jit(solution)/shard_map/ppermute | solution.py:27
  65.3 5.9 %collective-permute-start.6 = (f32[2,6,1,256]{3,0,2,1:T(2,128)}, f32[2,6,1,256]{3,0,2,1:T(2,128)}, u32[]{:S(2)}, u32[]{:S(2)}) collective-permute-start(f32[2,6,1,256]{3,0,2,1:T(2,128)} %copy.407), channel_id=1, source_target_pairs={{0,1},{1,2},{2,3},{4,5},{5,6},{6,7},{8,9},{9,10},{10,11},{12,13},{... | collective-permute-start | bytes 36872 | tf_op jit(solution)/shard_map/ppermute | solution.py:24
  71.2 1.1 %fusion.81 = (f32[1,6,18,64,4]{3,2,1,0,4:T(8,128)S(1)}, f32[1,6,18,64,4]{3,2,1,0,4:T(8,128)}, f32[1,6,18,64,4]{3,2,1,0,4:T(8,128)}, f32[1,6,18,64,4]{3,2,1,0,4:T...) fusion(f32[9,6,18,64,4]{3,2,1,0,4:T(8,128)S(1)} %pad_maximum_fusion), kind=kLoop, calls=%fused_computation.217 | loop fusion | bytes 1990656 | tf_op jit(solution)/shard_map/slice | solution.py:74
  73.3 1.3 %copy.354 = f32[1,6,18,64,4]{2,4,3,1,0:T(4,128)S(1)} copy(f32[1,6,18,64,4]{3,2,1,0,4:T(8,128)} %get-tuple-element.28) | data formatting | bytes 221184 | tf_op jit(solution)/shard_map/slice | solution.py:74
  75.2 0.8 copy.409
  75.9 1.3 %copy.350 = f32[1,6,18,64,4]{2,4,3,1,0:T(4,128)S(1)} copy(f32[1,6,18,64,4]{3,2,1,0,4:T(8,128)} %get-tuple-element.29) | data formatting | bytes 221184 | tf_op jit(solution)/shard_map/slice | solution.py:74
  77.5 0.9 copy.395
  78.5 1.3 %copy.346 = f32[1,6,18,64,4]{2,4,3,1,0:T(4,128)S(1)} copy(f32[1,6,18,64,4]{3,2,1,0,4:T(8,128)} %get-tuple-element.30) | data formatting | bytes 221184 | tf_op jit(solution)/shard_map/slice | solution.py:74
  80.0 0.9 copy.391
  81.6 0.9 copy.389
  82.5 0.4 copy.341
  83.4 0.8 copy.412
  84.2 1.3 %copy.340 = f32[1,6,18,64,4]{2,4,3,1,0:T(4,128)S(1)} copy(f32[1,6,18,64,4]{3,2,1,0,4:T(8,128)} %get-tuple-element.33) | data formatting | bytes 221184 | tf_op jit(solution)/shard_map/slice | solution.py:74
  86.0 0.8 copy.410
  86.8 0.4 copy.337
  87.6 0.8 copy.413
  88.4 1.3 %copy.336 = f32[1,6,18,64,4]{2,4,3,1,0:T(4,128)S(1)} copy(f32[1,6,18,64,4]{3,2,1,0,4:T(8,128)} %get-tuple-element.35) | data formatting | bytes 221184 | tf_op jit(solution)/shard_map/slice | solution.py:74
  90.3 0.7 copy.371
  91.0 0.7 copy.370
  91.8 1.0 pad_maximum_fusion.4
  92.7 1.3 %fusion.1 = (f32[6,6,18,256]{3,2,1,0:T(8,128)S(1)}, f32[1,6,18,256]{3,2,1,0:T(8,128)S(1)}, f32[1,6,18,256]{3,2,1,0:T(8,128)S(1)}, f32[1,6,18,256]{3,2,1,0:T(8,12...) fusion(f32[2,6,18,256]{3,2,1,0:T(8,128)S(1)} %pad_maximum_fusio, ...), kind=kLoop, calls=%fused_computation.31 | loop fusion | flops 1078271 | bytes 2543616
  94.0 0.6 fusion.7
  94.6 0.6 fusion.11
  95.3 0.6 fusion.3
  95.8 0.6 fusion.38
  96.4 0.6 fusion.9
  97.2 0.5 pad_maximum_fusion.1
  99.2 0.8 fusion.63
  (114 shorter events, 8.8 us)
Async XLA Ops:
  7.2 18.0 %all-to-all-start = ((s32[4,1,64]{2,1,0:T(1,128)}), s32[4,1,64]{2,1,0:T(1,128)S(1)}, u32[]{:S(2)}, u32[]{:S(2)}) async-start(s32[4,1,64]{2,1,0:T(1,128)} %and_select_fusion), calls=%async_computation | async-start | bytes 4096 | tf_op jit(solution)/shard_map/all_to_all | solution.py:223
  13.1 32.4 %collective-permute-start.9 = (f32[1,16,256]{2,1,0:T(8,128)S(1)}, f32[1,16,256]{2,1,0:T(8,128)S(1)}, u32[]{:S(2)}, u32[]{:S(2)}) collective-permute-start(f32[1,16,256]{2,1,0:T(8,128)S(1)} %get-tuple-element.89), channel_id=1, source_target_pairs={{4,0},{8,4},{12,8},{16,12},{20,16},{24,20},{28,24},{5,1},{9,5},{13... | collective-permute-start | bytes 49160 | tf_op jit(solution)/shard_map/ppermute | solution.py:27
  14.4 26.6 %collective-permute-start.8 = (f32[1,16,256]{2,1,0:T(8,128)S(1)}, f32[1,16,256]{2,1,0:T(8,128)S(1)}, u32[]{:S(2)}, u32[]{:S(2)}) collective-permute-start(f32[1,16,256]{2,1,0:T(8,128)S(1)} %get-tuple-element.90), channel_id=1, source_target_pairs={{0,4},{4,8},{8,12},{12,16},{16,20},{20,24},{24,28},{1,5},{5,9},{9,... | collective-permute-start | bytes 49160 | tf_op jit(solution)/shard_map/ppermute | solution.py:24
  18.2 44.4 %collective-permute-start.5 = (f32[2,1,16,256]{3,2,1,0:T(8,128)S(1)}, f32[2,1,16,256]{3,2,1,0:T(8,128)S(1)}, u32[]{:S(2)}, u32[]{:S(2)}) collective-permute-start(f32[2,1,16,256]{3,2,1,0:T(8,128)S(1)} %get-tuple-element.66), channel_id=1, source_target_pairs={{4,0},{8,4},{12,8},{16,12},{20,16},{24,20},{28,24},{5,1},{9,5},{13... | collective-permute-start | bytes 98312 | tf_op jit(solution)/shard_map/ppermute | solution.py:27
  19.5 42.5 %collective-permute-start.4 = (f32[2,1,16,256]{3,2,1,0:T(8,128)S(1)}, f32[2,1,16,256]{3,2,1,0:T(8,128)S(1)}, u32[]{:S(2)}, u32[]{:S(2)}) collective-permute-start(f32[2,1,16,256]{3,2,1,0:T(8,128)S(1)} %get-tuple-element.67), channel_id=1, source_target_pairs={{0,4},{4,8},{8,12},{12,16},{16,20},{20,24},{24,28},{1,5},{5,9},{9,... | collective-permute-start | bytes 98312 | tf_op jit(solution)/shard_map/ppermute | solution.py:24
  28.0 8.9 %all-to-all-start.1 = ((f32[4,1,576]{2,1,0:T(1,128)}), f32[4,1,576]{2,1,0:T(1,128)S(1)}, u32[]{:S(2)}, u32[]{:S(2)}) async-start(f32[4,1,576]{2,1,0:T(1,128)} %reshape.1544), calls=%async_computation.1 | async-start | bytes 20480 | tf_op jit(solution)/shard_map/all_to_all | solution.py:225
  39.7 8.4 %collective-permute-start.1 = (f32[9,1,4,64]{3,2,0,1:T(4,128)S(1)}, f32[9,1,4,64]{3,2,0,1:T(4,128)S(1)}, u32[]{:S(2)}, u32[]{:S(2)}) collective-permute-start(f32[9,1,4,64]{3,2,0,1:T(4,128)S(1)} %copy.323), channel_id=1, source_target_pairs={{4,0},{8,4},{12,8},{16,12},{20,16},{24,20},{28,24},{5,1},{9,5},{13... | collective-permute-start | bytes 27656 | tf_op jit(solution)/shard_map/ppermute | solution.py:27
  41.0 8.4 %collective-permute-start = (f32[9,1,4,64]{3,2,0,1:T(4,128)S(1)}, f32[9,1,4,64]{3,2,0,1:T(4,128)S(1)}, u32[]{:S(2)}, u32[]{:S(2)}) collective-permute-start(f32[9,1,4,64]{3,2,0,1:T(4,128)S(1)} %copy.323), channel_id=1, source_target_pairs={{0,4},{4,8},{8,12},{12,16},{16,20},{20,24},{24,28},{1,5},{5,9},{9,... | collective-permute-start | bytes 27656 | tf_op jit(solution)/shard_map/ppermute | solution.py:24
  45.6 8.4 %collective-permute-start.10 = (f32[6,1,256]{2,1,0:T(1,128)S(1)}, f32[6,1,256]{2,1,0:T(1,128)S(1)}, u32[]{:S(2)}, u32[]{:S(2)}) collective-permute-start(f32[6,1,256]{2,1,0:T(1,128)S(1)} %get-tuple-element.85), channel_id=1, source_target_pairs={{0,1},{1,2},{2,3},{4,5},{5,6},{6,7},{8,9},{9,10},{10,11},{12,13},{... | collective-permute-start | bytes 18440 | tf_op jit(solution)/shard_map/ppermute | solution.py:24
  48.1 7.2 %collective-permute-start.11 = (f32[6,1,256]{2,1,0:T(1,128)S(1)}, f32[6,1,256]{2,1,0:T(1,128)S(1)}, u32[]{:S(2)}, u32[]{:S(2)}) collective-permute-start(f32[6,1,256]{2,1,0:T(1,128)S(1)} %get-tuple-element.86), channel_id=1, source_target_pairs={{1,0},{2,1},{3,2},{5,4},{6,5},{7,6},{9,8},{10,9},{11,10},{13,12},{... | collective-permute-start | bytes 18440 | tf_op jit(solution)/shard_map/ppermute | solution.py:27
  49.4 6.7 %collective-permute-start.2 = (f32[9,3,1,64]{3,2,0,1:T(1,128)S(1)}, f32[9,3,1,64]{3,2,0,1:T(1,128)S(1)}, u32[]{:S(2)}, u32[]{:S(2)}) collective-permute-start(f32[9,3,1,64]{3,2,0,1:T(1,128)S(1)} %get-tuple-element.91), channel_id=1, source_target_pairs={{0,1},{1,2},{2,3},{4,5},{5,6},{6,7},{8,9},{9,10},{10,11},{12,13},{... | collective-permute-start | bytes 20744 | tf_op jit(solution)/shard_map/ppermute | solution.py:24
  54.0 6.1 %collective-permute-start.3 = (f32[9,3,1,64]{3,2,0,1:T(1,128)S(1)}, f32[9,3,1,64]{3,2,0,1:T(1,128)S(1)}, u32[]{:S(2)}, u32[]{:S(2)}) collective-permute-start(f32[9,3,1,64]{3,2,0,1:T(1,128)S(1)} %get-tuple-element.92), channel_id=1, source_target_pairs={{1,0},{2,1},{3,2},{5,4},{6,5},{7,6},{9,8},{10,9},{11,10},{13,12},{... | collective-permute-start | bytes 20744 | tf_op jit(solution)/shard_map/ppermute | solution.py:27
  61.8 0.9 copy-start.5
  62.7 2.6 %copy-start.4 = (f32[2,6,16,256]{3,2,1,0:T(8,128)}, f32[2,6,16,256]{3,2,1,0:T(8,128)S(1)}, u32[]{:S(2)}) copy-start(f32[2,6,16,256]{3,2,1,0:T(8,128)S(1)} %constant_dynamic-update-slice_fusion) | copy-start | bytes 589828
  64.0 26.3 %collective-permute-start.7 = (f32[2,6,1,256]{3,0,2,1:T(2,128)}, f32[2,6,1,256]{3,0,2,1:T(2,128)}, u32[]{:S(2)}, u32[]{:S(2)}) collective-permute-start(f32[2,6,1,256]{3,0,2,1:T(2,128)} %copy.408), channel_id=1, source_target_pairs={{1,0},{2,1},{3,2},{5,4},{6,5},{7,6},{9,8},{10,9},{11,10},{13,12},{... | collective-permute-start | bytes 36872 | tf_op jit(solution)/shard_map/ppermute | solution.py:27
  65.3 25.7 %collective-permute-start.6 = (f32[2,6,1,256]{3,0,2,1:T(2,128)}, f32[2,6,1,256]{3,0,2,1:T(2,128)}, u32[]{:S(2)}, u32[]{:S(2)}) collective-permute-start(f32[2,6,1,256]{3,0,2,1:T(2,128)} %copy.407), channel_id=1, source_target_pairs={{0,1},{1,2},{2,3},{4,5},{5,6},{6,7},{8,9},{9,10},{10,11},{12,13},{... | collective-permute-start | bytes 36872 | tf_op jit(solution)/shard_map/ppermute | solution.py:24
  97.2 0.8 copy-start.11
  97.8 0.7 copy-start.12
  97.8 1.0 copy-start.13
  97.8 1.2 %copy-start = (f32[6,18,256]{2,1,0:T(8,128)S(1)}, f32[6,18,256]{2,1,0:T(8,128)}, u32[]{:S(2)}) copy-start(f32[6,18,256]{2,1,0:T(8,128)} %copy.395) | copy-start | bytes 331780
  97.8 1.2 %copy-start.1 = (f32[6,18,256]{2,1,0:T(8,128)S(1)}, f32[6,18,256]{2,1,0:T(8,128)}, u32[]{:S(2)}) copy-start(f32[6,18,256]{2,1,0:T(8,128)} %copy.391) | copy-start | bytes 331780
  97.8 1.2 %copy-start.2 = (f32[6,18,256]{2,1,0:T(8,128)S(1)}, f32[6,18,256]{2,1,0:T(8,128)}, u32[]{:S(2)}) copy-start(f32[6,18,256]{2,1,0:T(8,128)} %copy.389) | copy-start | bytes 331780
  97.9 1.2 %copy-start.3 = (f32[4,16,256]{2,1,0:T(8,128)S(1)}, f32[4,16,256]{2,1,0:T(8,128)}, u32[]{:S(2)}) copy-start(f32[4,16,256]{2,1,0:T(8,128)} %param.5) | copy-start | bytes 196612
  97.9 1.2 %copy-start.6 = (f32[4,16,256]{2,1,0:T(8,128)S(1)}, f32[4,16,256]{2,1,0:T(8,128)}, u32[]{:S(2)}) copy-start(f32[4,16,256]{2,1,0:T(8,128)} %copy.409) | copy-start | bytes 196612
  97.9 1.2 %copy-start.7 = (f32[4,16,256]{2,1,0:T(8,128)S(1)}, f32[4,16,256]{2,1,0:T(8,128)}, u32[]{:S(2)}) copy-start(f32[4,16,256]{2,1,0:T(8,128)} %copy.412) | copy-start | bytes 196612
  97.9 1.2 %copy-start.8 = (f32[4,16,256]{2,1,0:T(8,128)S(1)}, f32[4,16,256]{2,1,0:T(8,128)}, u32[]{:S(2)}) copy-start(f32[4,16,256]{2,1,0:T(8,128)} %copy.410) | copy-start | bytes 196612
  97.9 1.2 %copy-start.9 = (f32[4,16,256]{2,1,0:T(8,128)S(1)}, f32[4,16,256]{2,1,0:T(8,128)}, u32[]{:S(2)}) copy-start(f32[4,16,256]{2,1,0:T(8,128)} %copy.413) | copy-start | bytes 196612
  98.0 1.2 %copy-start.10 = (f32[4,16,256]{2,1,0:T(8,128)S(1)}, f32[4,16,256]{2,1,0:T(8,128)}, u32[]{:S(2)}) copy-start(f32[4,16,256]{2,1,0:T(8,128)} %param.6) | copy-start | bytes 196612
where the time goes:
time: 101 us; the launch traced here: 99.9 us
  starting transfers between devices  39.8 us (39%)
  local copies, waits for them, and re-layouts  32.6 us (32%)
  other arithmetic  17.9 us (18%)
  waiting for transfers between devices  8.2 us (8%)
  between operations  1.42 us (1%)
    ppermute x6, starting transfers between devices, padded_2(): lax.ppermute(lax.slice_in_dim(block, block.shape[dim] - width, None, axis...  22.7 us
    slice x10, local copies, waits for them, and re-layouts, tensors(): entries = [field[number] for number in range(9)]  9.17 us
    ppermute x6, starting transfers between devices, padded_2(): lax.ppermute(lax.slice_in_dim(block, 0, width, axis=dim), axis, backward)  7.72 us
    unnamed x41, local copies, waits for them, and re-layouts  7.11 us
    squeeze x13, local copies, waits for them, and re-layouts, tensors(): entries = [field[number] for number in range(9)]  5.44 us
    all_to_all x1, starting transfers between devices, local(): lax.all_to_all(wanted, 'gy', split_axis=0, concat_axis=0, tiled=True)  5.19 us
    all_to_all x1, starting transfers between devices, local(): lax.all_to_all(picked, 'gy', split_axis=1, concat_axis=1, tiled=True)  4.19 us
    all_to_all x1, waiting for transfers between devices, local(): lax.all_to_all(picked, 'gy', split_axis=1, concat_axis=1, tiled=True)  4.19 us
  transfers between devices with their start and end apart: 14, of which 2 were waited for; matrix products, arithmetic and copies ran while one was open for 33% of the time, Pallas kernels for 0%

commit v1 on v0

v1 whole, which is shorter than its diff:
```python
import functools

import jax
import jax.numpy as jnp
import numpy as np
from jax import lax
from jax.experimental import pallas as pl
from jax.experimental.pallas import tpu as pltpu
from jax.sharding import PartitionSpec as P

RATIO = 4

sigma_fiber = 1.0
sigma_cross = 0.3
time_step = 0.1
excite_gain = 8.0
excite_level = 0.15
stretch_gain = 10.0
stretch_reversal = 0.6
recover_rate = 0.5


def round_up(value, multiple):
    return -(-value // multiple) * multiple


def interpolation(count):
    weights = np.zeros((RATIO * count + 2, count + 2))
    for cell in range(-1, RATIO * count + 1):
        element, position = cell // RATIO, cell % RATIO
        offset = (position + 0.5) / RATIO - 0.5
        weights[cell + 1, element + 1] += 1.0 - abs(offset)
        weights[cell + 1, element + 1 + (1 if offset > 0 else -1)] += abs(offset)
    return weights


def fit_series():
    nodes = np.cos((np.arange(64) + 0.5) * np.pi / 64)
    square = (nodes + 1.0) * 0.5 * np.pi**2
    root = np.sqrt(square)
    series = []
    for values in (np.sin(root) / root, np.cos(root)):
        fitted = np.polynomial.chebyshev.Chebyshev.fit(square, values, 8, domain=[0.0, np.pi**2])
        series.append(fitted.convert(kind=np.polynomial.Polynomial).coef)
    return series


SINE, COSINE = fit_series()


def horner(series, square):
    total = jnp.full_like(square, float(series[-1]))
    for coefficient in series[-2::-1]:
        total = total * square + float(coefficient)
    return total


def sine_cosine(angle):
    square = angle * angle
    return (angle * horner(SINE, square), horner(COSINE, square))


def parts_of(values, count):
    pieces = []
    for _ in range(count):
        piece = values.astype(jnp.bfloat16)
        pieces.append(piece)
        values = values - piece.astype(jnp.float32)
    return pieces


def dot(left, right):
    return jnp.dot(left, right, preferred_element_type=jnp.float32)


def fill_gradients(out_ref, start, deform_ref, slot_ref, row, rows):
    components, held = deform_ref.shape
    columns, depth = slot_ref.shape[1:]
    out_ref[start : start + rows, :] = jnp.zeros((rows, out_ref.shape[1]), jnp.float32)
    out_ref[start : start + components, 0:held] = deform_ref[...]
    out_ref[start + components : start + components + columns, 0:depth] = slot_ref[row].astype(
        jnp.float32
    )


def pack_x(potential_ref, angle_ref, deform_ref, slot_ref, down_ref, up_ref):
    cells_x, cells_y = potential_ref.shape[:2]
    for out_ref, cell, element in (
        (down_ref, 0, 0),
        (up_ref, cells_x - 1, slot_ref.shape[0] - 1),
    ):
        out_ref[0:cells_y] = potential_ref[cell]
        out_ref[cells_y : 2 * cells_y] = angle_ref[0, cell]
        out_ref[2 * cells_y : 3 * cells_y] = angle_ref[1, cell]
        fill_gradients(
            out_ref, 3 * cells_y, deform_ref, slot_ref, element, out_ref.shape[0] - 3 * cells_y
        )


def pack_y(
    potential_ref, angle_ref, deform_ref, slot_ref, down_ref, up_ref, low_ref, high_ref, out_ref
):
    cells_x, cells_y, depth = potential_ref.shape
    rows = low_ref.shape[0] - 3 * cells_y
    elements = slot_ref.shape[0]
    at_first = lax.axis_index("gx") == 0
    at_last = lax.axis_index("gx") == lax.axis_size("gx") - 1

    def low(start, stop):
        return jnp.where(at_first, down_ref[start:stop], low_ref[start:stop])

    def high(start, stop):
        return jnp.where(at_last, up_ref[start:stop], high_ref[start:stop])

    out_ref[0:rows] = low(3 * cells_y, 3 * cells_y + rows)
    for element in range(elements):
        fill_gradients(out_ref, (element + 1) * rows, deform_ref, slot_ref, element, rows)
    out_ref[(elements + 1) * rows : (elements + 2) * rows] = high(
        3 * cells_y, 3 * cells_y + rows
    )
    base = (elements + 2) * rows
    side_rows = (out_ref.shape[0] - base) // 2
    first_rows = round_up(cells_x + 2, 8)
    out_ref[base:, :] = jnp.zeros((2 * side_rows, depth), jnp.float32)
    for side, cell in ((0, 0), (1, cells_y - 1)):
        start = base + side * side_rows
        out_ref[start : start + 1] = low(cell, cell + 1)
        for x in range(cells_x):
            out_ref[start + 1 + x : start + 2 + x] = potential_ref[x, cell : cell + 1, :]
        out_ref[start + 1 + cells_x : start + 2 + cells_x] = high(cell, cell + 1)
        for kind in range(2):
            for x in range(cells_x):
                line = start + first_rows + kind * cells_x + x
                out_ref[line : line + 1] = angle_ref[kind, x, cell : cell + 1, :]


def tensors(entries, azimuth, elevation):
    sin_u, cos_u = sine_cosine(azimuth)
    sin_e, cos_e = sine_cosine(elevation)
    fiber = [cos_u * cos_e, sin_u * cos_e, sin_e]

    def element(row_index, col_index):
        return entries[3 * (row_index % 3) + col_index % 3]

    cofactor = [
        [
            element(row + 1, col + 1) * element(row + 2, col + 2)
            - element(row + 1, col + 2) * element(row + 2, col + 1)
            for col in range(3)
        ]
        for row in range(3)
    ]
    determinant = (
        element(0, 0) * cofactor[0][0]
        + element(0, 1) * cofactor[0][1]
        + element(0, 2) * cofactor[0][2]
    )
    scale = 1.0 / determinant
    adjugate = [[cofactor[col][row] for col in range(3)] for row in range(3)]
    pulled = [
        adjugate[row][0] * fiber[0] + adjugate[row][1] * fiber[1] + adjugate[row][2] * fiber[2]
        for row in range(3)
    ]
    cross = (scale * scale) * sigma_cross
    along = (scale * scale) * (sigma_fiber - sigma_cross)
    conduct = []
    for first, second in ((0, 0), (1, 1), (2, 2), (0, 1), (0, 2), (1, 2)):
        metric = (
            adjugate[first][0] * adjugate[second][0]
            + adjugate[first][1] * adjugate[second][1]
            + adjugate[first][2] * adjugate[second][2]
        )
        conduct.append(cross * metric + along * (pulled[first] * pulled[second]))
    return conduct, fiber


def stretch_of(entries, fiber):
    total = None
    for row in range(3):
        value = (
            entries[3 * row] * fiber[0]
            + entries[3 * row + 1] * fiber[1]
            + entries[3 * row + 2] * fiber[2]
        )
        total = value * value if total is None else total + value * value
    return jnp.sqrt(total)


def step(
    potential_ref,
    recovery_ref,
    angle_ref,
    down_ref,
    up_ref,
    low_ref,
    high_ref,
    row_ref,
    deep_ref,
    wide_ref,
    potential_out,
    recovery_out,
    coarse_ref,
    fine_ref,
    conduct_ref,
    stretch_ref,
    *,
    columns,
    coarse_depth,
    held,
    components,
):
    cells_x, cells_y, depth = potential_ref.shape
    devices = row_ref.shape[0]
    rows = low_ref.shape[0] - 3 * cells_y
    elements = cells_x // RATIO
    gx = lax.axis_index("gx")
    gy = lax.axis_index("gy")
    at_first_x = gx == 0
    at_last_x = gx == lax.axis_size("gx") - 1
    at_first_y = gy == 0
    at_last_y = gy == lax.axis_size("gy") - 1
    left = jnp.where(at_first_y, gy, gy - 1)
    right = jnp.where(at_last_y, gy, gy + 1)

    lanes = 2 * coarse_depth
    lane = lax.broadcasted_iota(jnp.int32, (1, lanes), 1)
    slot_lines = []
    for r in range(elements + 2):
        base = r * rows + components
        own = row_ref[gy, base : base + columns, 0:lanes]
        before = jnp.where(
            at_first_y, own[0:1], row_ref[left, base + columns - 1 : base + columns, 0:lanes]
        )
        after = jnp.where(
            at_last_y, own[columns - 1 : columns], row_ref[right, base : base + 1, 0:lanes]
        )
        line = [before] + [own[c : c + 1] for c in range(columns)] + [after]
        slot_lines.append(line)
    count = columns + 2
    gathered = [[None] * (count // 2) for _ in range(elements + 2)]
    for r in range(elements + 2):
        table = row_ref[:, r * rows : (r + 1) * rows, 0:held].reshape(devices * rows, held)
        table_parts = parts_of(table, 3)
        for pair in range(count // 2):
            slots = jnp.where(
                lane < coarse_depth,
                slot_lines[r][2 * pair],
                pltpu.roll(slot_lines[r][2 * pair + 1], coarse_depth, 1),
            ).astype(jnp.int32)
            place = slots % held
            holder = (slots // held) % devices
            match = lax.broadcasted_iota(jnp.int32, (held, lanes), 0) == place
            chosen = jnp.where(match, 1.0, 0.0).astype(jnp.bfloat16)
            values = dot(table_parts[0], chosen)
            for part in table_parts[1:]:
                values = values + dot(part, chosen)
            picked = values[0:rows]
            for device in range(1, devices):
                picked = jnp.where(
                    holder == device, values[device * rows : (device + 1) * rows], picked
                )
            gathered[r][pair] = picked

    tall = (elements + 2) * rows
    for pair in range(count // 2):
        stacked = jnp.concatenate([gathered[r][pair] for r in range(elements + 2)], axis=0)
        values = None
        for part in parts_of(stacked, 3):
            term = dot(part, deep_ref[...])
            values = term if values is None else values + term
        coarse_ref[2 * pair * tall : (2 * pair + 1) * tall] = values[:, 0:depth]
        coarse_ref[(2 * pair + 1) * tall : (2 * pair + 2) * tall] = values[:, depth : 2 * depth]
    coarse_parts = parts_of(coarse_ref[...], 2)
    fine_ref[...] = dot(wide_ref[...], coarse_parts[0]) + dot(wide_ref[...], coarse_parts[1])

    total_rows = fine_ref.shape[0] // components
    inner_rows = cells_x * cells_y
    base_y = (elements + 2) * rows
    side_rows = (row_ref.shape[1] - base_y) // 2
    first_rows = round_up(cells_x + 2, 8)
    left_start = pl.multiple_of(jnp.where(at_first_y, base_y, base_y + side_rows), 8)
    right_start = pl.multiple_of(jnp.where(at_last_y, base_y + side_rows, base_y), 8)
    chunk = 8
    for start in range(0, total_rows, chunk):
        entries = [
            fine_ref[k * total_rows + start : k * total_rows + start + chunk]
            for k in range(components)
        ]
        if start < inner_rows:
            x, y = start // cells_y, start % cells_y
            azimuth = angle_ref[0, x, y : y + chunk]
            elevation = angle_ref[1, x, y : y + chunk]
        elif start < inner_rows + 2 * cells_y:
            is_low = start < inner_rows + cells_y
            y = (start - inner_rows) % cells_y
            kinds = []
            for kind in range(2):
                line = (1 + kind) * cells_y + y
                own_ref, got_ref = (down_ref, low_ref) if is_low else (up_ref, high_ref)
                kinds.append(
                    jnp.where(
                        at_first_x if is_low else at_last_x,
                        own_ref[line : line + chunk],
                        got_ref[line : line + chunk],
                    )
                )
            azimuth, elevation = kinds
        else:
            left_angles = row_ref[left, pl.ds(left_start + first_rows, 2 * cells_x), :]
            right_angles = row_ref[right, pl.ds(right_start + first_rows, 2 * cells_x), :]
            azimuth = jnp.concatenate([left_angles[0:cells_x], right_angles[0:cells_x]], axis=0)
            elevation = jnp.concatenate([left_angles[cells_x:], right_angles[cells_x:]], axis=0)
        conduct, fiber = tensors(entries, azimuth, elevation)
        for number in range(6):
            conduct_ref[number, start : start + chunk] = conduct[number]
        if start < inner_rows:
            stretch_ref[start : start + chunk] = stretch_of(entries, fiber)

    row_index = lax.broadcasted_iota(jnp.int32, (cells_y, depth), 0)
    lane_index = lax.broadcasted_iota(jnp.int32, (cells_y, depth), 1)
    rim_low = row_ref[left, pl.ds(left_start, first_rows), :]
    rim_high = row_ref[right, pl.ds(right_start, first_rows), :]

    def deeper(values, first):
        return jnp.where(first, values, pltpu.roll(values, 1, 1))

    def grad_z(values):
        index = lax.broadcasted_iota(jnp.int32, values.shape, 1)
        after = jnp.where(index == depth - 1, values, pltpu.roll(values, depth - 1, 1))
        before = jnp.where(index == 0, values, pltpu.roll(values, 1, 1))
        return (after - before) * 0.5

    def lower_y(values, rim):
        return jnp.where(row_index == 0, rim, pltpu.roll(values, 1, 0))

    def upper_y(values, rim):
        return jnp.where(row_index == cells_y - 1, rim, pltpu.roll(values, cells_y - 1, 0))

    def voltage_at(x):
        if x < 0:
            return jnp.where(at_first_x, down_ref[0:cells_y], low_ref[0:cells_y])
        if x >= cells_x:
            return jnp.where(at_last_x, up_ref[0:cells_y], high_ref[0:cells_y])
        return potential_ref[x]

    def conduct_at(number, x):
        if x < 0:
            return conduct_ref[number, inner_rows : inner_rows + cells_y]
        if x >= cells_x:
            return conduct_ref[number, inner_rows + cells_y : inner_rows + 2 * cells_y]
        return conduct_ref[number, x * cells_y : (x + 1) * cells_y]

    voltages = [voltage_at(x) for x in range(-1, cells_x + 1)]
    grads_y = [
        (
            upper_y(voltages[x], rim_high[x : x + 1])
            - lower_y(voltages[x], rim_low[x : x + 1])
        )
        * 0.5
        for x in range(cells_x + 2)
    ]
    grads_z = [grad_z(values) for values in voltages]
    rim_z = [grad_z(rim_low), grad_z(rim_high)]

    def flux(tensor_a, tensor_b, grads_a, grads_b, straight, voltage_a, voltage_b):
        total = None
        for place in range(3):
            mean = (tensor_a[place] + tensor_b[place]) * 0.5
            if place == straight:
                term = mean * (voltage_b - voltage_a)
            else:
                term = mean * ((grads_a[place] + grads_b[place]) * 0.5)
            total = term if total is None else total + term
        return total

    flux_x = []
    for face in range(cells_x + 1):
        value = flux(
            [conduct_at(n, face - 1) for n in (0, 3, 4)],
            [conduct_at(n, face) for n in (0, 3, 4)],
            [None, grads_y[face], grads_z[face]],
            [None, grads_y[face + 1], grads_z[face + 1]],
            0,
            voltages[face],
            voltages[face + 1],
        )
        if face == 0:
            value = jnp.where(at_first_x, 0.0, value)
        if face == cells_x:
            value = jnp.where(at_last_x, 0.0, value)
        flux_x.append(value)

    rim_start = inner_rows + 2 * cells_y
    for x in range(cells_x):
        voltage = voltages[x + 1]
        grad_x = (voltages[x + 2] - voltages[x]) * 0.5
        grad_y = grads_y[x + 1]
        grad_zz = grads_z[x + 1]
        tensor = [conduct_at(n, x) for n in (3, 1, 5)]
        low_tensor = [conduct_ref[n, rim_start + x : rim_start + x + 1] for n in (3, 1, 5)]
        high_tensor = [
            conduct_ref[n, rim_start + cells_x + x : rim_start + cells_x + x + 1]
            for n in (3, 1, 5)
        ]
        low_grads = [
            (rim_low[x + 2 : x + 3] - rim_low[x : x + 1]) * 0.5,
            None,
            rim_z[0][x + 1 : x + 2],
        ]
        high_grads = [
            (rim_high[x + 2 : x + 3] - rim_high[x : x + 1]) * 0.5,
            None,
            rim_z[1][x + 1 : x + 2],
        ]
        lower = flux(
            [lower_y(tensor[n], low_tensor[n]) for n in range(3)],
            tensor,
            [lower_y(grad_x, low_grads[0]), None, lower_y(grad_zz, low_grads[2])],
            [grad_x, None, grad_zz],
            1,
            lower_y(voltage, rim_low[x + 1 : x + 2]),
            voltage,
        )
        lower = jnp.where((row_index == 0) & at_first_y, 0.0, lower)
        top = flux(
            [value[cells_y - 1 : cells_y] for value in tensor],
            high_tensor,
            [grad_x[cells_y - 1 : cells_y], None, grad_zz[cells_y - 1 : cells_y]],
            high_grads,
            1,
            voltage[cells_y - 1 : cells_y],
            rim_high[x + 1 : x + 2],
        )
        top = jnp.where(at_last_y, 0.0, top)
        divergent = flux_x[x + 1] - flux_x[x] + (upper_y(lower, top) - lower)
        first = lane_index == 0
        tensor = [conduct_at(n, x) for n in (4, 5, 2)]
        before = flux(
            [deeper(value, first) for value in tensor],
            tensor,
            [deeper(grad_x, first), deeper(grad_y, first), None],
            [grad_x, grad_y, None],
            2,
            deeper(voltage, first),
            voltage,
        )
        before = jnp.where(first, 0.0, before)
        divergent = divergent + (pltpu.roll(before, depth - 1, 1) - before)
        recovery = recovery_ref[x]
        stretch = stretch_ref[x * cells_y : (x + 1) * cells_y]
        current = (
            excite_gain * voltage * (voltage - excite_level) * (voltage - 1.0)
            + voltage * recovery
        )
        current = current + stretch_gain * jnp.maximum(stretch - 1.0, 0.0) * (
            voltage - stretch_reversal
        )
        potential_out[x] = voltage + time_step * (divergent - current)
        recovery_out[x] = recovery + time_step * recover_rate * (
            -recovery - excite_gain * voltage * (voltage - excite_level - 1.0)
        )


def weights_of(cells_x, cells_y, columns, coarse_depth, depth, rows, components):
    elements = cells_x // RATIO
    deep = np.zeros((coarse_depth, depth))
    along_z = interpolation(coarse_depth)[1:-1]
    deep += along_z[:, 1:-1].T
    deep[0] += along_z[:, 0]
    deep[-1] += along_z[:, -1]
    pair = np.zeros((2 * coarse_depth, 2 * depth))
    pair[:coarse_depth, :depth] = deep
    pair[coarse_depth:, depth:] = deep
    along_x = interpolation(elements)
    along_y = interpolation(columns)
    places = [(x + 1, y + 1) for x in range(cells_x) for y in range(cells_y)]
    places += [(x, y + 1) for x in (0, cells_x + 1) for y in range(cells_y)]
    places += [(x + 1, y) for y in (0, cells_y + 1) for x in range(cells_x)]
    wide = np.zeros((components, len(places), columns + 2, elements + 2, rows))
    for line, (x, y) in enumerate(places):
        block = along_y[y][:, None] * along_x[x][None, :]
        for k in range(components):
            wide[k, line, :, :, k] = block
    wide = wide.reshape(components * len(places), -1)
    return jnp.asarray(pair, jnp.bfloat16), jnp.asarray(wide, jnp.bfloat16), len(places)


def local(potential, recovery, fiber_angles, deform, elem_slot):
    cells_x, cells_y, depth = potential.shape
    elements, columns, coarse_depth = elem_slot.shape
    components, held = deform.shape
    rows = round_up(components + columns, 8)
    deep, wide, line_count = weights_of(
        cells_x, cells_y, columns, coarse_depth, depth, rows, components
    )
    packet = jax.ShapeDtypeStruct((3 * cells_y + rows, depth), jnp.float32)
    down, up = pl.pallas_call(pack_x, out_shape=(packet, packet), name="pack_x")(
        potential, fiber_angles, deform, elem_slot
    )
    forward = [(i, i + 1) for i in range(lax.axis_size("gx") - 1)]
    backward = [(target, source) for source, target in forward]
    low = lax.ppermute(up, "gx", forward)
    high = lax.ppermute(down, "gx", backward)
    sides = 2 * (round_up(cells_x + 2, 8) + 2 * cells_x)
    payload = pl.pallas_call(
        pack_y,
        out_shape=jax.ShapeDtypeStruct(((elements + 2) * rows + sides, depth), jnp.float32),
        name="pack_y",
    )(potential, fiber_angles, deform, elem_slot, down, up, low, high)
    row = lax.all_gather(payload, "gy", axis=0, tiled=False)
    block = jax.ShapeDtypeStruct((cells_x, cells_y, depth), jnp.float32)
    return pl.pallas_call(
        functools.partial(
            step, columns=columns, coarse_depth=coarse_depth, held=held, components=components
        ),
        out_shape=(block, block),
        scratch_shapes=[
            pltpu.VMEM(((columns + 2) * (elements + 2) * rows, depth), jnp.float32),
            pltpu.VMEM((components * line_count, depth), jnp.float32),
            pltpu.VMEM((6, line_count, depth), jnp.float32),
            pltpu.VMEM((cells_x * cells_y, depth), jnp.float32),
        ],
        name="step",
    )(potential, recovery, fiber_angles, down, up, low, high, row, deep, wide)


def solution(mesh):
    placed = (
        P("gx", "gy", None),
        P("gx", "gy", None),
        P(None, "gx", "gy", None),
        P(None, ("gx", "gy")),
        P("gx", "gy", None),
    )
    return jax.shard_map(
        local,
        mesh=mesh,
        in_specs=placed,
        out_specs=(P("gx", "gy", None), P("gx", "gy", None)),
        check_vma=False,
    )
```

time: 101 us -> 27.9 us (0.28)
  the two profiles are of different devices: /device:TPU:0 before, /device:TPU:24 now
where the time goes in v1:
time: 27.9 us; the launch traced here: 27.6 us
  blocking collectives  11 us (39%)
  Pallas kernels  7.63 us (27%)
  starting transfers between devices  4.31 us (15%)
  waiting for transfers between devices  3.36 us (12%)
  between operations  0.66 us (2%)
  local copies, waits for them, and re-layouts  0.62 us (2%)
    all_gather x1, blocking collectives, local(): row = lax.all_gather(payload, 'gy', axis=0, tiled=False)  11 us
    pallas_call x1, Pallas kernels, local(): pl.pallas_call(functools.partial(step, columns=columns, coarse_depth=coar...  4.35 us
    ppermute x1, waiting for transfers between devices, local(): low = lax.ppermute(up, 'gx', forward)  3.36 us
    ppermute x1, starting transfers between devices, local(): low = lax.ppermute(up, 'gx', forward)  2.4 us
    ppermute x1, starting transfers between devices, local(): high = lax.ppermute(down, 'gx', backward)  1.91 us
    pallas_call x1, Pallas kernels, local(): pl.pallas_call(pack_y, out_shape=jax.ShapeDtypeStruct(((elements + 2) * r...  1.71 us
    pallas_call x1, Pallas kernels, local(): pl.pallas_call(pack_x, out_shape=(packet, packet), name='pack_x')  1.57 us
    unnamed x4, local copies, waits for them, and re-layouts  0.62 us
  transfers between devices with their start and end apart: 2, of which 1 were waited for; matrix products, arithmetic and copies ran while one was open for 0% of the time, Pallas kernels for 0%

profile of v1, /device:TPU:24, one launch (start us, length us, event | category | flops | bytes accessed | tf_op | source)
XLA Modules:
  0.0 27.6 jit_solution(14996625484196767936)
XLA Ops:
  0.6 1.6 %pack_x.1 = (f32[64,256]{1,0:T(8,128)}, f32[64,256]{1,0:T(8,128)}) custom-call(f32[4,16,256]{2,1,0:T(8,128)} %potential_ref.5, f32[2,4,16,256]{3,2,1,0:T(8,128)} %angle_ref.5, f32[9,256]{1,0:T(8,128)} %deform_ref.3, s32[1,4,64]{2,1,0:T(4,128)} %slot_ref.3), custom_call_target="tpu_custom_call" | custom-call | tf_op jit(solution)/shard_map/pack_x/pallas_call | solution.py:497
  2.2 1.9 %collective-permute-start.1 = (f32[64,256]{1,0:T(8,128)}, f32[64,256]{1,0:T(8,128)S(1)}, u32[]{:S(2)}, u32[]{:S(2)}) collective-permute-start(f32[64,256]{1,0:T(8,128)} %get-tuple-element.4.down_ref), channel_id=1, source_target_pairs={{4,0},{8,4},{12,8},{16,12},{20,16},{24,20},{28,24},{5,1},{9,5},{13... | collective-permute-start | bytes 196616 | tf_op jit(solution)/shard_map/ppermute | solution.py:503
  4.1 2.4 %collective-permute-start = (f32[64,256]{1,0:T(8,128)}, f32[64,256]{1,0:T(8,128)S(1)}, u32[]{:S(2)}, u32[]{:S(2)}) collective-permute-start(f32[64,256]{1,0:T(8,128)} %get-tuple-element.5.up_ref), channel_id=1, source_target_pairs={{0,4},{4,8},{8,12},{12,16},{16,20},{20,24},{24,28},{1,5},{5,9},{9,... | collective-permute-start | bytes 196616 | tf_op jit(solution)/shard_map/ppermute | solution.py:502
  6.5 0.0 collective-permute-done.1.high_ref
  6.5 0.0 copy-start
  6.5 3.4 %collective-permute-done.low_ref = f32[64,256]{1,0:T(8,128)S(1)} collective-permute-done((f32[64,256]{1,0:T(8,128)}, f32[64,256]{1,0:T(8,128)S(1)}, u32[]{:S(2)}, u32[]{:S(2)}) %collective-permute-start) | collective-permute-done | bytes 65568 | tf_op jit(solution)/shard_map/ppermute | solution.py:502
  9.9 0.0 copy-done
  9.9 0.0 copy-start.1
  9.9 0.6 %copy-done.1 = f32[64,256]{1,0:T(8,128)} copy-done((f32[64,256]{1,0:T(8,128)}, f32[64,256]{1,0:T(8,128)S(1)}, u32[]{:S(2)}) %copy-start.1) | copy-done | bytes 65560
  10.5 1.7 %pack_y.1 = f32[80,256]{1,0:T(8,128)} custom-call(f32[4,16,256]{2,1,0:T(8,128)} %potential_ref.5, f32[2,4,16,256]{3,2,1,0:T(8,128)} %angle_ref.5, f32[9,256]{1,0:T(8,128)} %deform_ref.3, s32[1,4,64]{2,1,0:T(4,128)} %slot_ref.3, f32[64,256]{1,0:T(8,128)} %get-tuple-element.4.down_ref, f32[64,256]{1,0:T(8,128)} %get-tuple-element.5.up_ref, ...), custom_call_target="tpu_custom_call" | custom-call | tf_op jit(solution)/shard_map/pack_y/pallas_call | solution.py:505
  12.2 11.0 %all-gather = f32[320,256]{1,0:T(8,128)} all-gather(f32[80,256]{1,0:T(8,128)} %pack_y.1), channel_id=2, replica_groups=mesh['gx'=8,'gy'=4] {'gy'}, dimensions={0}, use_global_device_ids=true | all-gather | bytes 409600 | tf_op jit(solution)/shard_map/all_gather | solution.py:510
  23.3 4.3 %step.1 = (f32[4,16,256]{2,1,0:T(8,128)}, f32[4,16,256]{2,1,0:T(8,128)}) custom-call(f32[4,16,256]{2,1,0:T(8,128)} %potential_ref.5, f32[4,16,256]{2,1,0:T(8,128)} %recovery_ref.1, f32[2,4,16,256]{3,2,1,0:T(8,128)} %angle_ref.5, f32[64,256]{1,0:T(8,128)} %get-tuple-element.4.down_ref, f32[64,256]{1,0:T(8,128)} %get-tuple-element.5.up_ref, ...), custom_call_target="tpu_custom_call" | custom-call | tf_op jit(solution)/shard_map/step/pallas_call | solution.py:512
Async XLA Ops:
  2.2 4.3 %collective-permute-start.1 = (f32[64,256]{1,0:T(8,128)}, f32[64,256]{1,0:T(8,128)S(1)}, u32[]{:S(2)}, u32[]{:S(2)}) collective-permute-start(f32[64,256]{1,0:T(8,128)} %get-tuple-element.4.down_ref), channel_id=1, source_target_pairs={{4,0},{8,4},{12,8},{16,12},{20,16},{24,20},{28,24},{5,1},{9,5},{13... | collective-permute-start | bytes 196616 | tf_op jit(solution)/shard_map/ppermute | solution.py:503
  4.1 5.8 %collective-permute-start = (f32[64,256]{1,0:T(8,128)}, f32[64,256]{1,0:T(8,128)S(1)}, u32[]{:S(2)}, u32[]{:S(2)}) collective-permute-start(f32[64,256]{1,0:T(8,128)} %get-tuple-element.5.up_ref), channel_id=1, source_target_pairs={{0,4},{4,8},{8,12},{12,16},{16,20},{20,24},{24,28},{1,5},{5,9},{9,... | collective-permute-start | bytes 196616 | tf_op jit(solution)/shard_map/ppermute | solution.py:502
  6.5 3.4 %copy-start = (f32[64,256]{1,0:T(8,128)}, f32[64,256]{1,0:T(8,128)S(1)}, u32[]{:S(2)}) copy-start(f32[64,256]{1,0:T(8,128)S(1)} %collective-permute-done.1.high_ref) | copy-start | bytes 196612
  9.9 0.6 %copy-start.1 = (f32[64,256]{1,0:T(8,128)}, f32[64,256]{1,0:T(8,128)S(1)}, u32[]{:S(2)}) copy-start(f32[64,256]{1,0:T(8,128)S(1)} %collective-permute-done.low_ref) | copy-start | bytes 196612

commit v2 on v1

--- a/solution.py
+++ b/solution.py
@@ -9,6 +9,7 @@
 from jax.sharding import PartitionSpec as P
 
 RATIO = 4
+SAME, EVEN, ODD = 0, 1, 2
 
 sigma_fiber = 1.0
 sigma_cross = 0.3
@@ -73,65 +74,51 @@
     return jnp.dot(left, right, preferred_element_type=jnp.float32)
 
 
-def fill_gradients(out_ref, start, deform_ref, slot_ref, row, rows):
+def pack(potential_ref, angle_ref, deform_ref, slot_ref, *out_refs, keys, rows):
+    cells_x, cells_y = potential_ref.shape[:2]
     components, held = deform_ref.shape
-    columns, depth = slot_ref.shape[1:]
-    out_ref[start : start + rows, :] = jnp.zeros((rows, out_ref.shape[1]), jnp.float32)
-    out_ref[start : start + components, 0:held] = deform_ref[...]
-    out_ref[start + components : start + components + columns, 0:depth] = slot_ref[row].astype(
-        jnp.float32
-    )
-
-
-def pack_x(potential_ref, angle_ref, deform_ref, slot_ref, down_ref, up_ref):
-    cells_x, cells_y = potential_ref.shape[:2]
-    for out_ref, cell, element in (
-        (down_ref, 0, 0),
-        (up_ref, cells_x - 1, slot_ref.shape[0] - 1),
-    ):
-        out_ref[0:cells_y] = potential_ref[cell]
-        out_ref[cells_y : 2 * cells_y] = angle_ref[0, cell]
-        out_ref[2 * cells_y : 3 * cells_y] = angle_ref[1, cell]
-        fill_gradients(
-            out_ref, 3 * cells_y, deform_ref, slot_ref, element, out_ref.shape[0] - 3 * cells_y
-        )
-
-
-def pack_y(
-    potential_ref, angle_ref, deform_ref, slot_ref, down_ref, up_ref, low_ref, high_ref, out_ref
-):
-    cells_x, cells_y, depth = potential_ref.shape
-    rows = low_ref.shape[0] - 3 * cells_y
-    elements = slot_ref.shape[0]
-    at_first = lax.axis_index("gx") == 0
-    at_last = lax.axis_index("gx") == lax.axis_size("gx") - 1
-
-    def low(start, stop):
-        return jnp.where(at_first, down_ref[start:stop], low_ref[start:stop])
-
-    def high(start, stop):
-        return jnp.where(at_last, up_ref[start:stop], high_ref[start:stop])
-
-    out_ref[0:rows] = low(3 * cells_y, 3 * cells_y + rows)
-    for element in range(elements):
-        fill_gradients(out_ref, (element + 1) * rows, deform_ref, slot_ref, element, rows)
-    out_ref[(elements + 1) * rows : (elements + 2) * rows] = high(
-        3 * cells_y, 3 * cells_y + rows
-    )
-    base = (elements + 2) * rows
-    side_rows = (out_ref.shape[0] - base) // 2
-    first_rows = round_up(cells_x + 2, 8)
-    out_ref[base:, :] = jnp.zeros((2 * side_rows, depth), jnp.float32)
-    for side, cell in ((0, 0), (1, cells_y - 1)):
-        start = base + side * side_rows
-        out_ref[start : start + 1] = low(cell, cell + 1)
-        for x in range(cells_x):
-            out_ref[start + 1 + x : start + 2 + x] = potential_ref[x, cell : cell + 1, :]
-        out_ref[start + 1 + cells_x : start + 2 + cells_x] = high(cell, cell + 1)
-        for kind in range(2):
-            for x in range(cells_x):
-                line = start + first_rows + kind * cells_x + x
-                out_ref[line : line + 1] = angle_ref[kind, x, cell : cell + 1, :]
+    columns, coarse_depth = slot_ref.shape[1:]
+    gx = lax.axis_index("gx")
+    gy = lax.axis_index("gy")
+    for key, out_ref in zip(keys, out_refs):
+        kind, flips = key
+        goes_up = (gx % 2 == 0) if kind == EVEN else (gx % 2 == 1)
+        goes_right = (gy ^ flips) > gy
+        depth = out_ref.shape[1]
+        start = out_ref.shape[0] - rows
+        out_ref[start:, :] = jnp.zeros((rows, depth), jnp.float32)
+        out_ref[start : start + components, 0:held] = deform_ref[...]
+        out_ref[start + components : start + components + columns, 0:coarse_depth] = slot_ref[
+            0
+        ].astype(jnp.float32)
+        if kind == SAME:
+            if start:
+                out_ref[0:start, :] = jnp.zeros((start, depth), jnp.float32)
+                for x in range(cells_x):
+                    for line, source in (
+                        (x, potential_ref.at[x]),
+                        (cells_x + x, angle_ref.at[0, x]),
+                        (2 * cells_x + x, angle_ref.at[1, x]),
+                    ):
+                        out_ref[line : line + 1] = jnp.where(
+                            goes_right, source[cells_y - 1 : cells_y], source[0:1]
+                        )
+        elif flips == 0:
+            out_ref[0:cells_y] = jnp.where(goes_up, potential_ref[cells_x - 1], potential_ref[0])
+            for number in range(2):
+                first = (number + 1) * cells_y
+                out_ref[first : first + cells_y] = jnp.where(
+                    goes_up, angle_ref[number, cells_x - 1], angle_ref[number, 0]
+                )
+        else:
+            corner = start + components + columns
+            above = jnp.where(
+                goes_right, potential_ref[cells_x - 1, cells_y - 1 :], potential_ref[cells_x - 1, 0:1]
+            )
+            below = jnp.where(
+                goes_right, potential_ref[0, cells_y - 1 :], potential_ref[0, 0:1]
+            )
+            out_ref[corner : corner + 1] = jnp.where(goes_up, above, below)
 
 
 def tensors(entries, azimuth, elevation):
@@ -190,74 +177,130 @@
     potential_ref,
     recovery_ref,
     angle_ref,
-    down_ref,
-    up_ref,
-    low_ref,
-    high_ref,
-    row_ref,
+    deform_ref,
+    slot_ref,
     deep_ref,
     wide_ref,
-    potential_out,
-    recovery_out,
-    coarse_ref,
-    fine_ref,
-    conduct_ref,
-    stretch_ref,
-    *,
-    columns,
-    coarse_depth,
-    held,
-    components,
+    *refs,
+    keys,
+    rows,
 ):
+    packets = dict(zip(keys, refs))
+    (
+        potential_out,
+        recovery_out,
+        table_ref,
+        low_ref,
+        high_ref,
+        coarse_ref,
+        fine_ref,
+        conduct_ref,
+        stretch_ref,
+    ) = refs[len(keys) :]
     cells_x, cells_y, depth = potential_ref.shape
-    devices = row_ref.shape[0]
-    rows = low_ref.shape[0] - 3 * cells_y
-    elements = cells_x // RATIO
+    components, held = deform_ref.shape
+    elements, columns, coarse_depth = slot_ref.shape
+    devices = lax.axis_size("gy")
     gx = lax.axis_index("gx")
     gy = lax.axis_index("gy")
     at_first_x = gx == 0
     at_last_x = gx == lax.axis_size("gx") - 1
     at_first_y = gy == 0
-    at_last_y = gy == lax.axis_size("gy") - 1
-    left = jnp.where(at_first_y, gy, gy - 1)
-    right = jnp.where(at_last_y, gy, gy + 1)
+    at_last_y = gy == devices - 1
+    is_odd = gx % 2 == 1
+    rims = [flips for flips in range(1, devices) if flips & (flips + 1) == 0]
+
+    def beside(values, towards, own):
+        chosen = own
+        for flips, value in values.items():
+            chosen = jnp.where((gy ^ flips) == towards, value, chosen)
+        return chosen
+
+    table_ref[1, 0] = jnp.zeros((rows, held), jnp.float32)
+    table_ref[1, 0, 0:components] = deform_ref[...]
+    table_ref[1, 0, components : components + columns, 0:coarse_depth] = slot_ref[0].astype(
+        jnp.float32
+    )
+    for flips in range(devices):
+        if flips:
+            table_ref[1, flips] = packets[SAME, flips][-rows:, :]
+        own = table_ref[1, flips]
+        even = packets[EVEN, flips][-rows:, :]
+        odd = packets[ODD, flips][-rows:, :]
+        table_ref[0, flips] = jnp.where(at_first_x, own, jnp.where(is_odd, even, odd))
+        table_ref[2, flips] = jnp.where(at_last_x, own, jnp.where(is_odd, odd, even))
+    even_ref, odd_ref = packets[EVEN, 0], packets[ODD, 0]
+    for number in range(3):
+        first = number * cells_y
+        own = (potential_ref, angle_ref.at[0], angle_ref.at[1])[number]
+        even = even_ref[first : first + cells_y]
+        odd = odd_ref[first : first + cells_y]
+        low_ref[first : first + cells_y] = jnp.where(
+            at_first_x, own[0], jnp.where(is_odd, even, odd)
+        )
+        high_ref[first : first + cells_y] = jnp.where(
+            at_last_x, own[cells_x - 1], jnp.where(is_odd, odd, even)
+        )
+    corner = components + columns
+    rim_rows = []
+    for side, towards in ((0, gy - 1), (cells_y - 1, gy + 1)):
+        inner = [
+            beside(
+                {f: packets[SAME, f][x : x + 1] for f in rims},
+                towards,
+                potential_ref[x, side : side + 1],
+            )
+            for x in range(cells_x)
+        ]
+        ends = []
+        for row, edge_ref, at_edge, near in (
+            (0, low_ref, at_first_x, inner[0]),
+            (2, high_ref, at_last_x, inner[-1]),
+        ):
+            value = beside(
+                {f: table_ref[row, f, corner : corner + 1] for f in rims},
+                towards,
+                edge_ref[side : side + 1],
+            )
+            ends.append(jnp.where(at_edge, near, value))
+        filler = [jnp.zeros_like(inner[0])] * (round_up(cells_x + 2, 8) - cells_x - 2)
+        rim_rows.append(jnp.concatenate([ends[0]] + inner + [ends[1]] + filler, axis=0))
+    rim_low, rim_high = rim_rows
 
     lanes = 2 * coarse_depth
     lane = lax.broadcasted_iota(jnp.int32, (1, lanes), 1)
-    slot_lines = []
-    for r in range(elements + 2):
-        base = r * rows + components
-        own = row_ref[gy, base : base + columns, 0:lanes]
-        before = jnp.where(
-            at_first_y, own[0:1], row_ref[left, base + columns - 1 : base + columns, 0:lanes]
-        )
-        after = jnp.where(
-            at_last_y, own[columns - 1 : columns], row_ref[right, base : base + 1, 0:lanes]
-        )
-        line = [before] + [own[c : c + 1] for c in range(columns)] + [after]
-        slot_lines.append(line)
     count = columns + 2
     gathered = [[None] * (count // 2) for _ in range(elements + 2)]
     for r in range(elements + 2):
-        table = row_ref[:, r * rows : (r + 1) * rows, 0:held].reshape(devices * rows, held)
-        table_parts = parts_of(table, 3)
+        own = table_ref[r, 0, components : components + columns, 0:lanes]
+        last = components + columns - 1
+        before = beside(
+            {f: table_ref[r, f, last : last + 1, 0:lanes] for f in rims}, gy - 1, own[0:1]
+        )
+        after = beside(
+            {f: table_ref[r, f, components : components + 1, 0:lanes] for f in rims},
+            gy + 1,
+            own[columns - 1 : columns],
+        )
+        line = [before] + [own[c : c + 1] for c in range(columns)] + [after]
+        table_parts = parts_of(table_ref[r].reshape(devices * rows, held), 3)
         for pair in range(count // 2):
             slots = jnp.where(
                 lane < coarse_depth,
-                slot_lines[r][2 * pair],
-                pltpu.roll(slot_lines[r][2 * pair + 1], coarse_depth, 1),
+                line[2 * pair],
+                pltpu.roll(line[2 * pair + 1], coarse_depth, 1),
             ).astype(jnp.int32)
             place = slots % held
-            holder = (slots // held) % devices
+            flips_of = ((slots // held) % devices) ^ gy
             match = lax.broadcasted_iota(jnp.int32, (held, lanes), 0) == place
             chosen = jnp.where(match, 1.0, 0.0).astype(jnp.bfloat16)
             values = dot(table_parts[0], chosen)
             for part in table_parts[1:]:
                 values = values + dot(part, chosen)
             picked = values[0:rows]
-            for device in range(1, devices):
+            for flips in range(1, devices):
                 picked = jnp.where(
-                    holder == device, values[device * rows : (device + 1) * rows], picked
+                    flips_of == flips, values[flips * rows : (flips + 1) * rows], picked
                 )
             gathered[r][pair] = picked
 
@@ -275,11 +318,6 @@
 
     total_rows = fine_ref.shape[0] // components
     inner_rows = cells_x * cells_y
-    base_y = (elements + 2) * rows
-    side_rows = (row_ref.shape[1] - base_y) // 2
-    first_rows = round_up(cells_x + 2, 8)
-    left_start = pl.multiple_of(jnp.where(at_first_y, base_y, base_y + side_rows), 8)
-    right_start = pl.multiple_of(jnp.where(at_last_y, base_y + side_rows, base_y), 8)
     chunk = 8
     for start in range(0, total_rows, chunk):
         entries = [
@@ -291,25 +329,19 @@
             azimuth = angle_ref[0, x, y : y + chunk]
             elevation = angle_ref[1, x, y : y + chunk]
         elif start < inner_rows + 2 * cells_y:
-            is_low = start < inner_rows + cells_y
+            edge_ref = low_ref if start < inner_rows + cells_y else high_ref
             y = (start - inner_rows) % cells_y
-            kinds = []
-            for kind in range(2):
-                line = (1 + kind) * cells_y + y
-                own_ref, got_ref = (down_ref, low_ref) if is_low else (up_ref, high_ref)
-                kinds.append(
-                    jnp.where(
-                        at_first_x if is_low else at_last_x,
-                        own_ref[line : line + chunk],
-                        got_ref[line : line + chunk],
-                    )
-                )
-            azimuth, elevation = kinds
+            azimuth = edge_ref[cells_y + y : cells_y + y + chunk]
+            elevation = edge_ref[2 * cells_y + y : 2 * cells_y + y + chunk]
         else:
-            left_angles = row_ref[left, pl.ds(left_start + first_rows, 2 * cells_x), :]
-            right_angles = row_ref[right, pl.ds(right_start + first_rows, 2 * cells_x), :]
-            azimuth = jnp.concatenate([left_angles[0:cells_x], right_angles[0:cells_x]], axis=0)
-            elevation = jnp.concatenate([left_angles[cells_x:], right_angles[cells_x:]], axis=0)
+            pieces = [[], []]
+            for number in range(2):
+                first = (number + 1) * cells_x
+                for towards in (gy - 1, gy + 1):
+                    values = {f: packets[SAME, f][first : first + cells_x] for f in rims}
+                    pieces[number].append(beside(values, towards, values[rims[0]]))
+            azimuth = jnp.concatenate(pieces[0], axis=0)
+            elevation = jnp.concatenate(pieces[1], axis=0)
         conduct, fiber = tensors(entries, azimuth, elevation)
         for number in range(6):
             conduct_ref[number, start : start + chunk] = conduct[number]
@@ -318,9 +350,6 @@
 
     row_index = lax.broadcasted_iota(jnp.int32, (cells_y, depth), 0)
     lane_index = lax.broadcasted_iota(jnp.int32, (cells_y, depth), 1)
-    rim_low = row_ref[left, pl.ds(left_start, first_rows), :]
-    rim_high = row_ref[right, pl.ds(right_start, first_rows), :]
-
     def deeper(values, first):
         return jnp.where(first, values, pltpu.roll(values, 1, 1))
 
@@ -338,9 +367,9 @@
 
     def voltage_at(x):
         if x < 0:
-            return jnp.where(at_first_x, down_ref[0:cells_y], low_ref[0:cells_y])
+            return low_ref[0:cells_y]
         if x >= cells_x:
-            return jnp.where(at_last_x, up_ref[0:cells_y], high_ref[0:cells_y])
+            return high_ref[0:cells_y]
         return potential_ref[x]
 
     def conduct_at(number, x):
@@ -489,39 +518,64 @@
     cells_x, cells_y, depth = potential.shape
     elements, columns, coarse_depth = elem_slot.shape
     components, held = deform.shape
-    rows = round_up(components + columns, 8)
+    rows = round_up(components + columns + 1, 8)
     deep, wide, line_count = weights_of(
         cells_x, cells_y, columns, coarse_depth, depth, rows, components
     )
-    packet = jax.ShapeDtypeStruct((3 * cells_y + rows, depth), jnp.float32)
-    down, up = pl.pallas_call(pack_x, out_shape=(packet, packet), name="pack_x")(
-        potential, fiber_angles, deform, elem_slot
-    )
-    forward = [(i, i + 1) for i in range(lax.axis_size("gx") - 1)]
-    backward = [(target, source) for source, target in forward]
-    low = lax.ppermute(up, "gx", forward)
-    high = lax.ppermute(down, "gx", backward)
-    sides = 2 * (round_up(cells_x + 2, 8) + 2 * cells_x)
-    payload = pl.pallas_call(
-        pack_y,
-        out_shape=jax.ShapeDtypeStruct(((elements + 2) * rows + sides, depth), jnp.float32),
-        name="pack_y",
-    )(potential, fiber_angles, deform, elem_slot, down, up, low, high)
-    row = lax.all_gather(payload, "gy", axis=0, tiled=False)
+    across, down = lax.axis_size("gx"), lax.axis_size("gy")
+    assert elements == 1 and columns % 2 == 0 and held == depth
+    assert down & (down - 1) == 0 and down > 1 and rows > components + columns
+
+    keys = [(kind, flips) for kind in (EVEN, ODD, SAME) for flips in range(down)]
+    keys.remove((SAME, 0))
+
+    def is_rim(flips):
+        return flips and flips & (flips + 1) == 0
+
+    def sender(key):
+        return key if key[1] == 0 or is_rim(key[1]) else None
+
+    senders = [key for key in keys if sender(key)] + [None]
+    shapes = []
+    for key in senders:
+        extra = 0
+        if key is not None and key[0] == SAME:
+            extra = round_up(3 * cells_x, 8)
+        elif key is not None and key[1] == 0:
+            extra = 3 * cells_y
+        shapes.append(jax.ShapeDtypeStruct((extra + rows, depth), jnp.float32))
+    packed = pl.pallas_call(
+        functools.partial(
+            pack, keys=[(SAME, 0) if key is None else key for key in senders], rows=rows
+        ),
+        out_shape=shapes,
+        name="pack",
+    )(potential, fiber_angles, deform, elem_slot)
+    packed = dict(zip(senders, packed))
+
+    def pairs(kind, flips):
+        for x in range(across):
+            peer = x if kind == SAME else (x ^ 1 if kind == EVEN else ((x + 1) ^ 1) - 1)
+            if 0 <= peer < across:
+                for y in range(down):
+                    yield (x * down + y, peer * down + (y ^ flips))
+
+    got = [lax.ppermute(packed[sender(key)], ("gx", "gy"), list(pairs(*key))) for key in keys]
     block = jax.ShapeDtypeStruct((cells_x, cells_y, depth), jnp.float32)
     return pl.pallas_call(
-        functools.partial(
-            step, columns=columns, coarse_depth=coarse_depth, held=held, components=components
-        ),
+        functools.partial(step, keys=keys, rows=rows),
         out_shape=(block, block),
         scratch_shapes=[
+            pltpu.VMEM((elements + 2, down, rows, held), jnp.float32),
+            pltpu.VMEM((3 * cells_y, depth), jnp.float32),
+            pltpu.VMEM((3 * cells_y, depth), jnp.float32),
             pltpu.VMEM(((columns + 2) * (elements + 2) * rows, depth), jnp.float32),
             pltpu.VMEM((components * line_count, depth), jnp.float32),
             pltpu.VMEM((6, line_count, depth), jnp.float32),
             pltpu.VMEM((cells_x * cells_y, depth), jnp.float32),
         ],
         name="step",
-    )(potential, recovery, fiber_angles, down, up, low, high, row, deep, wide)
+    )(potential, recovery, fiber_angles, deform, elem_slot, deep, wide, *got)
 
 
 def solution(mesh):

time: 27.9 us -> 32.5 us (1.16)
  the two profiles are of different devices: /device:TPU:24 before, /device:TPU:1 now
where the time goes in v2:
time: 32.5 us; the launch traced here: 32.3 us
  starting transfers between devices  19.7 us (61%)
  Pallas kernels  5.95 us (18%)
  waiting for transfers between devices  4.63 us (14%)
  local copies, waits for them, and re-layouts  1.19 us (4%)
  between operations  0.8 us (2%)
    ppermute x11, starting transfers between devices, local(): lax.ppermute(packed[sender(key)], ('gx', 'gy'), list(pairs(*key)))  19.7 us
    ppermute x11, waiting for transfers between devices, local(): lax.ppermute(packed[sender(key)], ('gx', 'gy'), list(pairs(*key)))  4.63 us
    pallas_call x1, Pallas kernels, local(): pl.pallas_call(functools.partial(step, keys=keys, rows=rows), out_shape=(...  4.31 us
    pallas_call x1, Pallas kernels, local(): pl.pallas_call(functools.partial(pack, keys=[(SAME, 0) if key is None els...  1.64 us
    unnamed x24, local copies, waits for them, and re-layouts  1.19 us
  transfers between devices with their start and end apart: 11, of which 3 were waited for; matrix products, arithmetic and copies ran while one was open for 0% of the time, Pallas kernels for 0%

profile of v2, /device:TPU:1, one launch (start us, length us, event | category | flops | bytes accessed | tf_op | source)
XLA Modules:
  0.0 32.3 jit_solution(11870556024211231913)
XLA Ops:
  0.6 1.6 %pack.1 = (f32[64,256]{1,0:T(8,128)}, f32[16,256]{1,0:T(8,128)}, f32[16,256]{1,0:T(8,128)}, f32[64,256]{1,0:T(8,128)}, f32[16,256]{1,0:T(8,128)}, /*index=5*/f32...) custom-call(f32[4,16,256]{2,1,0:T(8,128)} %potential_ref.3, f32[2,4,16,256]{3,2,1,0:T(8,128)} %angle_ref.3, ...), custom_call_target="tpu_custom_call" | custom-call | tf_op jit(solution)/shard_map/pack/pallas_call | solution.py:547
  2.3 0.0 copy-start.11
  2.3 2.7 %collective-permute-start.1 = (f32[16,256]{1,0:T(8,128)}, f32[16,256]{1,0:T(8,128)S(1)}, u32[]{:S(2)}, u32[]{:S(2)}) collective-permute-start(f32[16,256]{1,0:T(8,128)} %get-tuple-element.12), channel_id=1, source_target_pairs={{0,5},{1,4},{2,7},{3,6},{4,1},{5,0},{6,3},{7,2},{8,13},{9,12},{10,... | collective-permute-start | bytes 49160 | tf_op jit(solution)/shard_map/ppermute | solution.py:563
  4.9 1.0 %collective-permute-start.3 = (f32[16,256]{1,0:T(8,128)}, f32[16,256]{1,0:T(8,128)S(1)}, u32[]{:S(2)}, u32[]{:S(2)}) collective-permute-start(f32[16,256]{1,0:T(8,128)} %get-tuple-element.14), channel_id=1, source_target_pairs={{0,7},{1,6},{2,5},{3,4},{4,3},{5,2},{6,1},{7,0},{8,15},{9,14},{10,... | collective-permute-start | bytes 49160 | tf_op jit(solution)/shard_map/ppermute | solution.py:563
  6.0 0.6 %collective-permute-start = (f32[64,256]{1,0:T(8,128)}, f32[64,256]{1,0:T(8,128)S(1)}, u32[]{:S(2)}, u32[]{:S(2)}) collective-permute-start(f32[64,256]{1,0:T(8,128)} %get-tuple-element.11), channel_id=1, source_target_pairs={{0,4},{1,5},{2,6},{3,7},{4,0},{5,1},{6,2},{7,3},{8,12},{9,13},{10,... | collective-permute-start | bytes 196616 | tf_op jit(solution)/shard_map/ppermute | solution.py:563
  6.5 3.1 %collective-permute-start.4 = (f32[64,256]{1,0:T(8,128)}, f32[64,256]{1,0:T(8,128)S(1)}, u32[]{:S(2)}, u32[]{:S(2)}) collective-permute-start(f32[64,256]{1,0:T(8,128)} %get-tuple-element.15), channel_id=1, source_target_pairs={{4,8},{5,9},{6,10},{7,11},{8,4},{9,5},{10,6},{11,7},{12,16},{13,17... | collective-permute-start | bytes 196616 | tf_op jit(solution)/shard_map/ppermute | solution.py:563
  9.6 3.4 %collective-permute-start.5 = (f32[16,256]{1,0:T(8,128)}, f32[16,256]{1,0:T(8,128)S(1)}, u32[]{:S(2)}, u32[]{:S(2)}) collective-permute-start(f32[16,256]{1,0:T(8,128)} %get-tuple-element.16), channel_id=1, source_target_pairs={{4,9},{5,8},{6,11},{7,10},{8,5},{9,4},{10,7},{11,6},{12,17},{13,16... | collective-permute-start | bytes 49160 | tf_op jit(solution)/shard_map/ppermute | solution.py:563
  13.0 0.0 collective-permute-done.1.refs_1_
  13.0 0.0 copy-start.4
  13.0 3.0 %collective-permute-start.7 = (f32[16,256]{1,0:T(8,128)}, f32[16,256]{1,0:T(8,128)S(1)}, u32[]{:S(2)}, u32[]{:S(2)}) collective-permute-start(f32[16,256]{1,0:T(8,128)} %get-tuple-element.17), channel_id=1, source_target_pairs={{4,11},{5,10},{6,9},{7,8},{8,7},{9,6},{10,5},{11,4},{12,19},{13,18... | collective-permute-start | bytes 49160 | tf_op jit(solution)/shard_map/ppermute | solution.py:563
  16.1 0.0 collective-permute-done.3.refs_3_
  16.1 0.0 copy-start.5
  16.1 1.3 %collective-permute-start.9 = (f32[16,256]{1,0:T(8,128)}, f32[16,256]{1,0:T(8,128)S(1)}, u32[]{:S(2)}, u32[]{:S(2)}) collective-permute-start(f32[16,256]{1,0:T(8,128)} %get-tuple-element.13), channel_id=1, source_target_pairs={{0,2},{1,3},{2,0},{3,1},{4,6},{5,7},{6,4},{7,5},{8,10},{9,11},{10,... | collective-permute-start | bytes 49160 | tf_op jit(solution)/shard_map/ppermute | solution.py:563
  17.4 0.0 collective-permute-done.5.refs_5_
  17.4 0.0 copy-start.6
  17.4 2.2 %collective-permute-start.6 = (f32[16,256]{1,0:T(8,128)}, f32[16,256]{1,0:T(8,128)S(1)}, u32[]{:S(2)}, u32[]{:S(2)}) collective-permute-start(f32[16,256]{1,0:T(8,128)} %get-tuple-element.13), channel_id=1, source_target_pairs={{4,10},{5,11},{6,8},{7,9},{8,6},{9,7},{10,4},{11,5},{12,18},{13,19... | collective-permute-start | bytes 49160 | tf_op jit(solution)/shard_map/ppermute | solution.py:563
  19.6 0.5 %collective-permute-done.7.refs_7_ = f32[16,256]{1,0:T(8,128)S(1)} collective-permute-done((f32[16,256]{1,0:T(8,128)}, f32[16,256]{1,0:T(8,128)S(1)}, u32[]{:S(2)}, u32[]{:S(2)}) %collective-permute-start.7) | collective-permute-done | bytes 16416 | tf_op jit(solution)/shard_map/ppermute | solution.py:563
  20.1 0.0 copy-start.7
  20.1 1.3 %collective-permute-start.8 = (f32[32,256]{1,0:T(8,128)}, f32[32,256]{1,0:T(8,128)S(1)}, u32[]{:S(2)}, u32[]{:S(2)}) collective-permute-start(f32[32,256]{1,0:T(8,128)} %get-tuple-element.18), channel_id=1, source_target_pairs={{0,1},{1,0},{2,3},{3,2},{4,5},{5,4},{6,7},{7,6},{8,9},{9,8},{10,11... | collective-permute-start | bytes 98312 | tf_op jit(solution)/shard_map/ppermute | solution.py:563
  21.4 0.0 collective-permute-done.9.refs_9_
  21.4 0.0 copy-start.8
  21.4 1.2 %collective-permute-start.10 = (f32[32,256]{1,0:T(8,128)}, f32[32,256]{1,0:T(8,128)S(1)}, u32[]{:S(2)}, u32[]{:S(2)}) collective-permute-start(f32[32,256]{1,0:T(8,128)} %get-tuple-element.19), channel_id=1, source_target_pairs={{0,3},{1,2},{2,1},{3,0},{4,7},{5,6},{6,5},{7,4},{8,11},{9,10},{10,... | collective-permute-start | bytes 98312 | tf_op jit(solution)/shard_map/ppermute | solution.py:563
  22.6 1.0 %collective-permute-done.6.refs_6_ = f32[16,256]{1,0:T(8,128)S(1)} collective-permute-done((f32[16,256]{1,0:T(8,128)}, f32[16,256]{1,0:T(8,128)S(1)}, u32[]{:S(2)}, u32[]{:S(2)}) %collective-permute-start.6) | collective-permute-done | bytes 16416 | tf_op jit(solution)/shard_map/ppermute | solution.py:563
  23.6 0.0 copy-done.11
  23.6 0.0 copy-start.9
  23.6 0.0 collective-permute-start.2
  23.6 3.2 %collective-permute-done.2.refs_2_ = f32[16,256]{1,0:T(8,128)S(1)} collective-permute-done((f32[16,256]{1,0:T(8,128)S(1)}, f32[16,256]{1,0:T(8,128)S(1)}, u32[]{:S(2)}, u32[]{:S(2)}) %collective-permute-start.2) | collective-permute-done | bytes 16416 | tf_op jit(solution)/shard_map/ppermute | solution.py:563
  26.7 0.0 copy-start.10
  26.7 0.0 collective-permute-done.8.refs_8_
  26.7 0.0 copy-start.2
  26.7 0.0 collective-permute-done.10.refs_10_
  26.7 0.0 copy-start.3
  26.7 0.0 collective-permute-done.refs_0_
  26.8 0.0 copy-start
  26.8 0.0 collective-permute-done.4.refs_4_
  26.8 0.0 copy-done.4
  26.8 0.0 copy-done.5
  26.8 0.0 copy-done.6
  26.8 0.0 copy-done.7
  26.8 0.0 copy-done.8
  26.8 0.0 copy-done.9
  26.8 0.5 %copy-done.10 = f32[16,256]{1,0:T(8,128)} copy-done((f32[16,256]{1,0:T(8,128)}, f32[16,256]{1,0:T(8,128)S(1)}, u32[]{:S(2)}) %copy-start.10) | copy-done | bytes 16408
  27.3 0.0 copy-done.2
  27.3 0.0 copy-done.3
  27.4 0.0 copy-done
  27.4 0.0 copy-start.1
  27.4 0.6 %copy-done.1 = f32[64,256]{1,0:T(8,128)} copy-done((f32[64,256]{1,0:T(8,128)}, f32[64,256]{1,0:T(8,128)S(1)}, u32[]{:S(2)}) %copy-start.1) | copy-done | bytes 65560
  28.0 4.3 %step.1 = (f32[4,16,256]{2,1,0:T(8,128)}, f32[4,16,256]{2,1,0:T(8,128)}) custom-call(f32[4,16,256]{2,1,0:T(8,128)} %potential_ref.3, f32[4,16,256]{2,1,0:T(8,128)} %recovery_ref.1, f32[2,4,16,256]{3,2,1,0:T(8,128)} %angle_ref.3, f32[9,256]{1,0:T(8,128)} %deform_ref.3, s32[1,4,64]{2,1,0:T(4,128)} %slot_ref.3, bf16[128,512]{1,0:T(8,128)(2,1)} %constant.4.clone.deep_ref, ...), custom_call_target="tpu_custom_call" | custom-call | tf_op jit(solution)/shard_map/step/pallas_call | solution.py:565
Async XLA Ops:
  2.3 21.3 %copy-start.11 = (f32[16,256]{1,0:T(8,128)S(1)}, f32[16,256]{1,0:T(8,128)}, u32[]{:S(2)}) copy-start(f32[16,256]{1,0:T(8,128)} %get-tuple-element.13) | copy-start | bytes 49156
  2.3 10.8 %collective-permute-start.1 = (f32[16,256]{1,0:T(8,128)}, f32[16,256]{1,0:T(8,128)S(1)}, u32[]{:S(2)}, u32[]{:S(2)}) collective-permute-start(f32[16,256]{1,0:T(8,128)} %get-tuple-element.12), channel_id=1, source_target_pairs={{0,5},{1,4},{2,7},{3,6},{4,1},{5,0},{6,3},{7,2},{8,13},{9,12},{10,... | collective-permute-start | bytes 49160 | tf_op jit(solution)/shard_map/ppermute | solution.py:563
  4.9 11.1 %collective-permute-start.3 = (f32[16,256]{1,0:T(8,128)}, f32[16,256]{1,0:T(8,128)S(1)}, u32[]{:S(2)}, u32[]{:S(2)}) collective-permute-start(f32[16,256]{1,0:T(8,128)} %get-tuple-element.14), channel_id=1, source_target_pairs={{0,7},{1,6},{2,5},{3,4},{4,3},{5,2},{6,1},{7,0},{8,15},{9,14},{10,... | collective-permute-start | bytes 49160 | tf_op jit(solution)/shard_map/ppermute | solution.py:563
  6.0 20.8 %collective-permute-start = (f32[64,256]{1,0:T(8,128)}, f32[64,256]{1,0:T(8,128)S(1)}, u32[]{:S(2)}, u32[]{:S(2)}) collective-permute-start(f32[64,256]{1,0:T(8,128)} %get-tuple-element.11), channel_id=1, source_target_pairs={{0,4},{1,5},{2,6},{3,7},{4,0},{5,1},{6,2},{7,3},{8,12},{9,13},{10,... | collective-permute-start | bytes 196616 | tf_op jit(solution)/shard_map/ppermute | solution.py:563
  6.5 20.2 %collective-permute-start.4 = (f32[64,256]{1,0:T(8,128)}, f32[64,256]{1,0:T(8,128)S(1)}, u32[]{:S(2)}, u32[]{:S(2)}) collective-permute-start(f32[64,256]{1,0:T(8,128)} %get-tuple-element.15), channel_id=1, source_target_pairs={{4,8},{5,9},{6,10},{7,11},{8,4},{9,5},{10,6},{11,7},{12,16},{13,17... | collective-permute-start | bytes 196616 | tf_op jit(solution)/shard_map/ppermute | solution.py:563
  9.6 7.8 %collective-permute-start.5 = (f32[16,256]{1,0:T(8,128)}, f32[16,256]{1,0:T(8,128)S(1)}, u32[]{:S(2)}, u32[]{:S(2)}) collective-permute-start(f32[16,256]{1,0:T(8,128)} %get-tuple-element.16), channel_id=1, source_target_pairs={{4,9},{5,8},{6,11},{7,10},{8,5},{9,4},{10,7},{11,6},{12,17},{13,16... | collective-permute-start | bytes 49160 | tf_op jit(solution)/shard_map/ppermute | solution.py:563
  13.0 13.7 %copy-start.4 = (f32[16,256]{1,0:T(8,128)}, f32[16,256]{1,0:T(8,128)S(1)}, u32[]{:S(2)}) copy-start(f32[16,256]{1,0:T(8,128)S(1)} %collective-permute-done.1.refs_1_) | copy-start | bytes 49156
  13.0 7.1 %collective-permute-start.7 = (f32[16,256]{1,0:T(8,128)}, f32[16,256]{1,0:T(8,128)S(1)}, u32[]{:S(2)}, u32[]{:S(2)}) collective-permute-start(f32[16,256]{1,0:T(8,128)} %get-tuple-element.17), channel_id=1, source_target_pairs={{4,11},{5,10},{6,9},{7,8},{8,7},{9,6},{10,5},{11,4},{12,19},{13,18... | collective-permute-start | bytes 49160 | tf_op jit(solution)/shard_map/ppermute | solution.py:563
  16.1 10.7 %copy-start.5 = (f32[16,256]{1,0:T(8,128)}, f32[16,256]{1,0:T(8,128)S(1)}, u32[]{:S(2)}) copy-start(f32[16,256]{1,0:T(8,128)S(1)} %collective-permute-done.3.refs_3_) | copy-start | bytes 49156
  16.1 5.3 %collective-permute-start.9 = (f32[16,256]{1,0:T(8,128)}, f32[16,256]{1,0:T(8,128)S(1)}, u32[]{:S(2)}, u32[]{:S(2)}) collective-permute-start(f32[16,256]{1,0:T(8,128)} %get-tuple-element.13), channel_id=1, source_target_pairs={{0,2},{1,3},{2,0},{3,1},{4,6},{5,7},{6,4},{7,5},{8,10},{9,11},{10,... | collective-permute-start | bytes 49160 | tf_op jit(solution)/shard_map/ppermute | solution.py:563
  17.4 9.4 %copy-start.6 = (f32[16,256]{1,0:T(8,128)}, f32[16,256]{1,0:T(8,128)S(1)}, u32[]{:S(2)}) copy-start(f32[16,256]{1,0:T(8,128)S(1)} %collective-permute-done.5.refs_5_) | copy-start | bytes 49156
  17.4 6.2 %collective-permute-start.6 = (f32[16,256]{1,0:T(8,128)}, f32[16,256]{1,0:T(8,128)S(1)}, u32[]{:S(2)}, u32[]{:S(2)}) collective-permute-start(f32[16,256]{1,0:T(8,128)} %get-tuple-element.13), channel_id=1, source_target_pairs={{4,10},{5,11},{6,8},{7,9},{8,6},{9,7},{10,4},{11,5},{12,18},{13,19... | collective-permute-start | bytes 49160 | tf_op jit(solution)/shard_map/ppermute | solution.py:563
  20.1 6.7 %copy-start.7 = (f32[16,256]{1,0:T(8,128)}, f32[16,256]{1,0:T(8,128)S(1)}, u32[]{:S(2)}) copy-start(f32[16,256]{1,0:T(8,128)S(1)} %collective-permute-done.7.refs_7_) | copy-start | bytes 49156
  20.1 6.6 %collective-permute-start.8 = (f32[32,256]{1,0:T(8,128)}, f32[32,256]{1,0:T(8,128)S(1)}, u32[]{:S(2)}, u32[]{:S(2)}) collective-permute-start(f32[32,256]{1,0:T(8,128)} %get-tuple-element.18), channel_id=1, source_target_pairs={{0,1},{1,0},{2,3},{3,2},{4,5},{5,4},{6,7},{7,6},{8,9},{9,8},{10,11... | collective-permute-start | bytes 98312 | tf_op jit(solution)/shard_map/ppermute | solution.py:563
  21.4 5.4 %copy-start.8 = (f32[16,256]{1,0:T(8,128)}, f32[16,256]{1,0:T(8,128)S(1)}, u32[]{:S(2)}) copy-start(f32[16,256]{1,0:T(8,128)S(1)} %collective-permute-done.9.refs_9_) | copy-start | bytes 49156
  21.4 5.3 %collective-permute-start.10 = (f32[32,256]{1,0:T(8,128)}, f32[32,256]{1,0:T(8,128)S(1)}, u32[]{:S(2)}, u32[]{:S(2)}) collective-permute-start(f32[32,256]{1,0:T(8,128)} %get-tuple-element.19), channel_id=1, source_target_pairs={{0,3},{1,2},{2,1},{3,0},{4,7},{5,6},{6,5},{7,4},{8,11},{9,10},{10,... | collective-permute-start | bytes 98312 | tf_op jit(solution)/shard_map/ppermute | solution.py:563
  23.6 3.3 %copy-start.9 = (f32[16,256]{1,0:T(8,128)}, f32[16,256]{1,0:T(8,128)S(1)}, u32[]{:S(2)}) copy-start(f32[16,256]{1,0:T(8,128)S(1)} %collective-permute-done.6.refs_6_) | copy-start | bytes 49156
  23.6 3.2 %collective-permute-start.2 = (f32[16,256]{1,0:T(8,128)S(1)}, f32[16,256]{1,0:T(8,128)S(1)}, u32[]{:S(2)}, u32[]{:S(2)}) collective-permute-start(f32[16,256]{1,0:T(8,128)S(1)} %copy-done.11), channel_id=1, source_target_pairs={{0,6},{1,7},{2,4},{3,5},{4,2},{5,3},{6,0},{7,1},{8,14},{9,15},{10,... | collective-permute-start | bytes 49160 | tf_op jit(solution)/shard_map/ppermute | solution.py:563
  26.7 0.6 %copy-start.10 = (f32[16,256]{1,0:T(8,128)}, f32[16,256]{1,0:T(8,128)S(1)}, u32[]{:S(2)}) copy-start(f32[16,256]{1,0:T(8,128)S(1)} %collective-permute-done.2.refs_2_) | copy-start | bytes 49156
  26.7 0.6 %copy-start.2 = (f32[32,256]{1,0:T(8,128)}, f32[32,256]{1,0:T(8,128)S(1)}, u32[]{:S(2)}) copy-start(f32[32,256]{1,0:T(8,128)S(1)} %collective-permute-done.8.refs_8_) | copy-start | bytes 98308
  26.7 0.6 %copy-start.3 = (f32[32,256]{1,0:T(8,128)}, f32[32,256]{1,0:T(8,128)S(1)}, u32[]{:S(2)}) copy-start(f32[32,256]{1,0:T(8,128)S(1)} %collective-permute-done.10.refs_10_) | copy-start | bytes 98308
  26.8 0.6 %copy-start = (f32[64,256]{1,0:T(8,128)}, f32[64,256]{1,0:T(8,128)S(1)}, u32[]{:S(2)}) copy-start(f32[64,256]{1,0:T(8,128)S(1)} %collective-permute-done.refs_0_) | copy-start | bytes 196612
  27.4 0.6 %copy-start.1 = (f32[64,256]{1,0:T(8,128)}, f32[64,256]{1,0:T(8,128)S(1)}, u32[]{:S(2)}) copy-start(f32[64,256]{1,0:T(8,128)S(1)} %collective-permute-done.4.refs_4_) | copy-start | bytes 196612

commit v3 on v2

--- a/solution.py
+++ b/solution.py
@@ -9,7 +9,6 @@
 from jax.sharding import PartitionSpec as P
 
 RATIO = 4
-SAME, EVEN, ODD = 0, 1, 2
 
 sigma_fiber = 1.0
 sigma_cross = 0.3
@@ -19,6 +18,14 @@
 stretch_gain = 10.0
 stretch_reversal = 0.6
 recover_rate = 0.5
+
+
+def IN(values):
+    return pltpu.with_memory_space_constraint(values, pltpu.VMEM)
+
+
+def OUT(shape):
+    return pltpu.VMEM(shape, jnp.float32)
 
 
 def round_up(value, multiple):
@@ -74,51 +81,63 @@
     return jnp.dot(left, right, preferred_element_type=jnp.float32)
 
 
-def pack(potential_ref, angle_ref, deform_ref, slot_ref, *out_refs, keys, rows):
-    cells_x, cells_y = potential_ref.shape[:2]
+def fill_gradients(out_ref, start, deform_ref, slot_ref, rows):
     components, held = deform_ref.shape
     columns, coarse_depth = slot_ref.shape[1:]
+    out_ref[start : start + rows, :] = jnp.zeros((rows, out_ref.shape[1]), jnp.float32)
+    out_ref[start : start + components, 0:held] = deform_ref[...]
+    out_ref[start + components : start + components + columns, 0:coarse_depth] = slot_ref[
+        0
+    ].astype(jnp.float32)
+
+
+def pack_x(potential_ref, angle_ref, deform_ref, slot_ref, even_ref, odd_ref, *, rows):
+    cells_x, cells_y = potential_ref.shape[:2]
+    gx = lax.axis_index("gx")
+    for out_ref, goes_up in ((even_ref, gx % 2 == 0), (odd_ref, gx % 2 == 1)):
+        sources = (potential_ref, angle_ref.at[0], angle_ref.at[1])
+        for number, source in enumerate(sources):
+            out_ref[number * cells_y : (number + 1) * cells_y] = jnp.where(
+                goes_up, source[cells_x - 1], source[0]
+            )
+        fill_gradients(out_ref, 3 * cells_y, deform_ref, slot_ref, rows)
+
+
+def pack_y(
+    potential_ref, angle_ref, deform_ref, slot_ref, even_ref, odd_ref, *out_refs, rims, rows
+):
+    low_ref, high_ref, row_ref = out_refs[:3]
+    cells_x, cells_y, depth = potential_ref.shape
     gx = lax.axis_index("gx")
     gy = lax.axis_index("gy")
-    for key, out_ref in zip(keys, out_refs):
-        kind, flips = key
-        goes_up = (gx % 2 == 0) if kind == EVEN else (gx % 2 == 1)
+    at_first = gx == 0
+    at_last = gx == lax.axis_size("gx") - 1
+    is_odd = gx % 2 == 1
+    fill_gradients(row_ref, rows, deform_ref, slot_ref, rows)
+    even, odd = even_ref[3 * cells_y :], odd_ref[3 * cells_y :]
+    own = row_ref[rows : 2 * rows]
+    row_ref[0:rows] = jnp.where(at_first, own, jnp.where(is_odd, even, odd))
+    row_ref[2 * rows :] = jnp.where(at_last, own, jnp.where(is_odd, odd, even))
+    for number, source in enumerate((potential_ref, angle_ref.at[0], angle_ref.at[1])):
+        part = slice(number * cells_y, (number + 1) * cells_y)
+        even, odd = even_ref[part], odd_ref[part]
+        low_ref[part] = jnp.where(at_first, source[0], jnp.where(is_odd, even, odd))
+        high_ref[part] = jnp.where(at_last, source[cells_x - 1], jnp.where(is_odd, odd, even))
+    first_rows = round_up(cells_x + 2, 8)
+    for flips, out_ref in zip(rims, out_refs[3:]):
         goes_right = (gy ^ flips) > gy
-        depth = out_ref.shape[1]
-        start = out_ref.shape[0] - rows
-        out_ref[start:, :] = jnp.zeros((rows, depth), jnp.float32)
-        out_ref[start : start + components, 0:held] = deform_ref[...]
-        out_ref[start + components : start + components + columns, 0:coarse_depth] = slot_ref[
-            0
-        ].astype(jnp.float32)
-        if kind == SAME:
-            if start:
-                out_ref[0:start, :] = jnp.zeros((start, depth), jnp.float32)
-                for x in range(cells_x):
-                    for line, source in (
-                        (x, potential_ref.at[x]),
-                        (cells_x + x, angle_ref.at[0, x]),
-                        (2 * cells_x + x, angle_ref.at[1, x]),
-                    ):
-                        out_ref[line : line + 1] = jnp.where(
-                            goes_right, source[cells_y - 1 : cells_y], source[0:1]
-                        )
-        elif flips == 0:
-            out_ref[0:cells_y] = jnp.where(goes_up, potential_ref[cells_x - 1], potential_ref[0])
-            for number in range(2):
-                first = (number + 1) * cells_y
-                out_ref[first : first + cells_y] = jnp.where(
-                    goes_up, angle_ref[number, cells_x - 1], angle_ref[number, 0]
-                )
-        else:
-            corner = start + components + columns
-            above = jnp.where(
-                goes_right, potential_ref[cells_x - 1, cells_y - 1 :], potential_ref[cells_x - 1, 0:1]
+        start = out_ref.shape[0] - 3 * rows
+        out_ref[start:] = row_ref[...]
+        out_ref[0:start] = jnp.zeros((start, depth), jnp.float32)
+        lines = [(0, low_ref), (1 + cells_x, high_ref)]
+        for x in range(cells_x):
+            lines.append((1 + x, potential_ref.at[x]))
+            lines.append((first_rows + x, angle_ref.at[0, x]))
+            lines.append((first_rows + cells_x + x, angle_ref.at[1, x]))
+        for line, source in lines:
+            out_ref[line : line + 1] = jnp.where(
+                goes_right, source[cells_y - 1 : cells_y], source[0:1]
             )
-            below = jnp.where(
-                goes_right, potential_ref[0, cells_y - 1 :], potential_ref[0, 0:1]
-            )
-            out_ref[corner : corner + 1] = jnp.where(goes_up, above, below)
 
 
 def tensors(entries, azimuth, elevation):
@@ -177,38 +196,37 @@
     potential_ref,
     recovery_ref,
     angle_ref,
-    deform_ref,
-    slot_ref,
+    low_ref,
+    high_ref,
+    line_ref,
+    side_ref,
     deep_ref,
-    wide_ref,
     *refs,
-    keys,
+    components,
+    held,
+    columns,
+    coarse_depth,
     rows,
+    devices,
 ):
-    packets = dict(zip(keys, refs))
+    packets = refs[:devices]
     (
         potential_out,
         recovery_out,
-        table_ref,
-        low_ref,
-        high_ref,
         coarse_ref,
         fine_ref,
         conduct_ref,
         stretch_ref,
-    ) = refs[len(keys) :]
+    ) = refs[devices:]
     cells_x, cells_y, depth = potential_ref.shape
-    components, held = deform_ref.shape
-    elements, columns, coarse_depth = slot_ref.shape
-    devices = lax.axis_size("gy")
+    elements = cells_x // RATIO
     gx = lax.axis_index("gx")
     gy = lax.axis_index("gy")
     at_first_x = gx == 0
     at_last_x = gx == lax.axis_size("gx") - 1
     at_first_y = gy == 0
     at_last_y = gy == devices - 1
-    is_odd = gx % 2 == 1
-    rims = [flips for flips in range(1, devices) if flips & (flips + 1) == 0]
+    rims = [flips for flips in range(1, devices) if is_rim(flips)]
 
     def beside(values, towards, own):
         chosen = own
@@ -216,55 +234,18 @@
             chosen = jnp.where((gy ^ flips) == towards, value, chosen)
         return chosen
 
-    table_ref[1, 0] = jnp.zeros((rows, held), jnp.float32)
-    table_ref[1, 0, 0:components] = deform_ref[...]
-    table_ref[1, 0, components : components + columns, 0:coarse_depth] = slot_ref[0].astype(
-        jnp.float32
-    )
-    for flips in range(devices):
-        if flips:
-            table_ref[1, flips] = packets[SAME, flips][-rows:, :]
-        own = table_ref[1, flips]
-        even = packets[EVEN, flips][-rows:, :]
-        odd = packets[ODD, flips][-rows:, :]
-        table_ref[0, flips] = jnp.where(at_first_x, own, jnp.where(is_odd, even, odd))
-        table_ref[2, flips] = jnp.where(at_last_x, own, jnp.where(is_odd, odd, even))
-    even_ref, odd_ref = packets[EVEN, 0], packets[ODD, 0]
-    for number in range(3):
-        first = number * cells_y
-        own = (potential_ref, angle_ref.at[0], angle_ref.at[1])[number]
-        even = even_ref[first : first + cells_y]
-        odd = odd_ref[first : first + cells_y]
-        low_ref[first : first + cells_y] = jnp.where(
-            at_first_x, own[0], jnp.where(is_odd, even, odd)
-        )
-        high_ref[first : first + cells_y] = jnp.where(
-            at_last_x, own[cells_x - 1], jnp.where(is_odd, odd, even)
-        )
-    corner = components + columns
+    def table(r, flips):
+        start = packets[flips].shape[0] - (elements + 2 - r) * rows
+        return packets[flips].at[start : start + rows]
+
+    first_rows = round_up(cells_x + 2, 8)
     rim_rows = []
     for side, towards in ((0, gy - 1), (cells_y - 1, gy + 1)):
-        inner = [
-            beside(
-                {f: packets[SAME, f][x : x + 1] for f in rims},
-                towards,
-                potential_ref[x, side : side + 1],
-            )
-            for x in range(cells_x)
-        ]
-        ends = []
-        for row, edge_ref, at_edge, near in (
-            (0, low_ref, at_first_x, inner[0]),
-            (2, high_ref, at_last_x, inner[-1]),
-        ):
-            value = beside(
-                {f: table_ref[row, f, corner : corner + 1] for f in rims},
-                towards,
-                edge_ref[side : side + 1],
-            )
-            ends.append(jnp.where(at_edge, near, value))
-        filler = [jnp.zeros_like(inner[0])] * (round_up(cells_x + 2, 8) - cells_x - 2)
-        rim_rows.append(jnp.concatenate([ends[0]] + inner + [ends[1]] + filler, axis=0))
+        sources = [low_ref] + [potential_ref.at[x] for x in range(cells_x)] + [high_ref]
+        own = [source[side : side + 1] for source in sources]
+        own += [jnp.zeros_like(own[0])] * (first_rows - len(own))
+        values = {flips: packets[flips][0:first_rows] for flips in rims}
+        rim_rows.append(beside(values, towards, jnp.concatenate(own, axis=0)))
     rim_low, rim_high = rim_rows
 
     lanes = 2 * coarse_depth
@@ -272,18 +253,20 @@
     count = columns + 2
     gathered = [[None] * (count // 2) for _ in range(elements + 2)]
     for r in range(elements + 2):
-        own = table_ref[r, 0, components : components + columns, 0:lanes]
+        own = table(r, 0)[components : components + columns, 0:lanes]
         last = components + columns - 1
         before = beside(
-            {f: table_ref[r, f, last : last + 1, 0:lanes] for f in rims}, gy - 1, own[0:1]
+            {f: table(r, f)[last : last + 1, 0:lanes] for f in rims}, gy - 1, own[0:1]
         )
         after = beside(
-            {f: table_ref[r, f, components : components + 1, 0:lanes] for f in rims},
+            {f: table(r, f)[components : components + 1, 0:lanes] for f in rims},
             gy + 1,
             own[columns - 1 : columns],
         )
         line = [before] + [own[c : c + 1] for c in range(columns)] + [after]
-        table_parts = parts_of(table_ref[r].reshape(devices * rows, held), 3)
+        table_parts = parts_of(
+            jnp.concatenate([table(r, f)[:, 0:held] for f in range(devices)], axis=0), 3
+        )
         for pair in range(count // 2):
             slots = jnp.where(
                 lane < coarse_depth,
@@ -313,16 +296,44 @@
             values = term if values is None else values + term
         coarse_ref[2 * pair * tall : (2 * pair + 1) * tall] = values[:, 0:depth]
         coarse_ref[(2 * pair + 1) * tall : (2 * pair + 2) * tall] = values[:, depth : 2 * depth]
-    coarse_parts = parts_of(coarse_ref[...], 2)
-    fine_ref[...] = dot(wide_ref[...], coarse_parts[0]) + dot(wide_ref[...], coarse_parts[1])
+    block_rows = cells_y * components
+    along_x = interpolation(elements)
+    blended = []
+    for x in range(cells_x + 2):
+        columns_x = []
+        for c in range(count):
+            total = None
+            for r in range(elements + 2):
+                weight = float(along_x[x, r])
+                if weight:
+                    start = c * tall + r * rows
+                    term = weight * coarse_ref[start : start + rows]
+                    total = term if total is None else total + term
+            columns_x.append(total)
+        pieces = parts_of(jnp.concatenate(columns_x, axis=0), 2)
+        blended.append(pieces)
+        place = x - 1 if 0 < x <= cells_x else (cells_x if x == 0 else cells_x + 1)
+        fine_ref[place * block_rows : (place + 1) * block_rows] = dot(
+            line_ref[...], pieces[0]
+        ) + dot(line_ref[...], pieces[1])
+    side_base = (cells_x + 2) * block_rows
+    total = None
+    for number in range(2):
+        stacked = jnp.concatenate([blended[x + 1][number] for x in range(cells_x)], axis=0)
+        term = dot(side_ref[...], stacked)
+        total = term if total is None else total + term
+    fine_ref[side_base:] = total
 
     total_rows = fine_ref.shape[0] // components
     inner_rows = cells_x * cells_y
     chunk = 8
     for start in range(0, total_rows, chunk):
+        if start < inner_rows + 2 * cells_y:
+            base, stride = start // cells_y * block_rows + start % cells_y, cells_y
+        else:
+            base, stride = side_base, total_rows - inner_rows - 2 * cells_y
         entries = [
-            fine_ref[k * total_rows + start : k * total_rows + start + chunk]
-            for k in range(components)
+            fine_ref[base + k * stride : base + k * stride + chunk] for k in range(components)
         ]
         if start < inner_rows:
             x, y = start // cells_y, start % cells_y
@@ -336,9 +347,9 @@
         else:
             pieces = [[], []]
             for number in range(2):
-                first = (number + 1) * cells_x
+                first = first_rows + number * cells_x
                 for towards in (gy - 1, gy + 1):
-                    values = {f: packets[SAME, f][first : first + cells_x] for f in rims}
+                    values = {f: packets[f][first : first + cells_x] for f in rims}
                     pieces[number].append(beside(values, towards, values[rims[0]]))
             azimuth = jnp.concatenate(pieces[0], axis=0)
             elevation = jnp.concatenate(pieces[1], axis=0)
@@ -491,7 +502,6 @@
 
 
 def weights_of(cells_x, cells_y, columns, coarse_depth, depth, rows, components):
-    elements = cells_x // RATIO
     deep = np.zeros((coarse_depth, depth))
     along_z = interpolation(coarse_depth)[1:-1]
     deep += along_z[:, 1:-1].T
@@ -500,18 +510,21 @@
     pair = np.zeros((2 * coarse_depth, 2 * depth))
     pair[:coarse_depth, :depth] = deep
     pair[coarse_depth:, depth:] = deep
-    along_x = interpolation(elements)
     along_y = interpolation(columns)
-    places = [(x + 1, y + 1) for x in range(cells_x) for y in range(cells_y)]
-    places += [(x, y + 1) for x in (0, cells_x + 1) for y in range(cells_y)]
-    places += [(x + 1, y) for y in (0, cells_y + 1) for x in range(cells_x)]
-    wide = np.zeros((components, len(places), columns + 2, elements + 2, rows))
-    for line, (x, y) in enumerate(places):
-        block = along_y[y][:, None] * along_x[x][None, :]
-        for k in range(components):
-            wide[k, line, :, :, k] = block
-    wide = wide.reshape(components * len(places), -1)
-    return jnp.asarray(pair, jnp.bfloat16), jnp.asarray(wide, jnp.bfloat16), len(places)
+    line = np.zeros((components, cells_y, columns + 2, rows))
+    side = np.zeros((components, 2, cells_x, cells_x, columns + 2, rows))
+    for k in range(components):
+        line[k, :, :, k] = along_y[1:-1]
+        for x in range(cells_x):
+            side[k, 0, x, x, :, k] = along_y[0]
+            side[k, 1, x, x, :, k] = along_y[-1]
+    line = line.reshape(components * cells_y, -1)
+    side = side.reshape(components * 2 * cells_x, -1)
+    return [jnp.asarray(values, jnp.bfloat16) for values in (line, side, pair)]
+
+
+def is_rim(flips):
+    return flips > 0 and flips & (flips + 1) == 0
 
 
 def local(potential, recovery, fiber_angles, deform, elem_slot):
@@ -519,63 +532,58 @@
     elements, columns, coarse_depth = elem_slot.shape
     components, held = deform.shape
     rows = round_up(components + columns + 1, 8)
-    deep, wide, line_count = weights_of(
-        cells_x, cells_y, columns, coarse_depth, depth, rows, components
-    )
+    weights = weights_of(cells_x, cells_y, columns, coarse_depth, depth, rows, components)
     across, down = lax.axis_size("gx"), lax.axis_size("gy")
     assert elements == 1 and columns % 2 == 0 and held == depth
-    assert down & (down - 1) == 0 and down > 1 and rows > components + columns
-
-    keys = [(kind, flips) for kind in (EVEN, ODD, SAME) for flips in range(down)]
-    keys.remove((SAME, 0))
-
-    def is_rim(flips):
-        return flips and flips & (flips + 1) == 0
-
-    def sender(key):
-        return key if key[1] == 0 or is_rim(key[1]) else None
-
-    senders = [key for key in keys if sender(key)] + [None]
-    shapes = []
-    for key in senders:
-        extra = 0
-        if key is not None and key[0] == SAME:
-            extra = round_up(3 * cells_x, 8)
-        elif key is not None and key[1] == 0:
-            extra = 3 * cells_y
-        shapes.append(jax.ShapeDtypeStruct((extra + rows, depth), jnp.float32))
-    packed = pl.pallas_call(
+    assert down & (down - 1) == 0 and down > 1 and 2 * cells_x == 8
+
+    def packet(count):
+        return OUT((count, depth))
+
+    arrays = (potential, fiber_angles, deform, elem_slot)
+    even, odd = pl.pallas_call(
+        functools.partial(pack_x, rows=rows),
+        out_shape=[packet(3 * cells_y + rows)] * 2,
+        name="pack_x",
+    )(*arrays)
+    even = lax.ppermute(even, "gx", [(x, x ^ 1) for x in range(across) if x ^ 1 < across])
+    upward = [(x, x + 1) for x in range(1, across - 1, 2)]
+    odd = lax.ppermute(odd, "gx", upward + [(high, low) for low, high in upward])
+    rims = [flips for flips in range(1, down) if is_rim(flips)]
+    side_rows = round_up(cells_x + 2, 8) + 2 * cells_x
+    low, high, row, *sent = pl.pallas_call(
+        functools.partial(pack_y, rims=rims, rows=rows),
+        out_shape=[packet(3 * cells_y)] * 2
+        + [packet(3 * rows)]
+        + [packet(side_rows + 3 * rows)] * len(rims),
+        name="pack_y",
+    )(*arrays, IN(even), IN(odd))
+    sent = dict(zip(rims, sent))
+    packets = [IN(row)]
+    for flips in range(1, down):
+        pairs = [(y, y ^ flips) for y in range(down)]
+        packets.append(IN(lax.ppermute(sent.get(flips, row), "gy", pairs)))
+    block = jax.ShapeDtypeStruct((cells_x, cells_y, depth), jnp.float32)
+    line_count = (cells_x + 2) * cells_y + 2 * cells_x
+    return pl.pallas_call(
         functools.partial(
-            pack, keys=[(SAME, 0) if key is None else key for key in senders], rows=rows
+            step,
+            components=components,
+            held=held,
+            columns=columns,
+            coarse_depth=coarse_depth,
+            rows=rows,
+            devices=down,
         ),
-        out_shape=shapes,
-        name="pack",
-    )(potential, fiber_angles, deform, elem_slot)
-    packed = dict(zip(senders, packed))
-
-    def pairs(kind, flips):
-        for x in range(across):
-            peer = x if kind == SAME else (x ^ 1 if kind == EVEN else ((x + 1) ^ 1) - 1)
-            if 0 <= peer < across:
-                for y in range(down):
-                    yield (x * down + y, peer * down + (y ^ flips))
-
-    got = [lax.ppermute(packed[sender(key)], ("gx", "gy"), list(pairs(*key))) for key in keys]
-    block = jax.ShapeDtypeStruct((cells_x, cells_y, depth), jnp.float32)
-    return pl.pallas_call(
-        functools.partial(step, keys=keys, rows=rows),
         out_shape=(block, block),
         scratch_shapes=[
-            pltpu.VMEM((elements + 2, down, rows, held), jnp.float32),
-            pltpu.VMEM((3 * cells_y, depth), jnp.float32),
-            pltpu.VMEM((3 * cells_y, depth), jnp.float32),
             pltpu.VMEM(((columns + 2) * (elements + 2) * rows, depth), jnp.float32),
             pltpu.VMEM((components * line_count, depth), jnp.float32),
             pltpu.VMEM((6, line_count, depth), jnp.float32),
             pltpu.VMEM((cells_x * cells_y, depth), jnp.float32),
         ],
         name="step",
-    )(potential, recovery, fiber_angles, deform, elem_slot, deep, wide, *got)
+    )(potential, recovery, fiber_angles, IN(low), IN(high), *weights, *packets)
 
 
 def solution(mesh):

time: 32.5 us -> 19.9 us (0.61)
  the two profiles are of different devices: /device:TPU:1 before, /device:TPU:17 now
where the time goes in v3:
time: 19.9 us; the launch traced here: 19.8 us
  waiting for transfers between devices  7.05 us (35%)
  starting transfers between devices  6.56 us (33%)
  Pallas kernels  5.5 us (28%)
  between operations  0.66 us (3%)
    ppermute x3, waiting for transfers between devices, local(): packets.append(IN(lax.ppermute(sent.get(flips, row), 'gy', pairs)))  4.6 us
    pallas_call x1, Pallas kernels, local(): pl.pallas_call(functools.partial(step, components=components, held=held,...  3.63 us
    ppermute x1, starting transfers between devices, local(): lax.ppermute(odd, 'gx', upward + [(high, low) for low, high in upward])  3.1 us
    ppermute x3, starting transfers between devices, local(): packets.append(IN(lax.ppermute(sent.get(flips, row), 'gy', pairs)))  2.71 us
    ppermute x1, waiting for transfers between devices, local(): lax.ppermute(odd, 'gx', upward + [(high, low) for low, high in upward])  2.45 us
    pallas_call x1, Pallas kernels, local(): pl.pallas_call(functools.partial(pack_y, rims=rims, rows=rows), out_shape...  0.95 us
    pallas_call x1, Pallas kernels, local(): pl.pallas_call(functools.partial(pack_x, rows=rows), out_shape=[packet(3...  0.93 us
    ppermute x1, starting transfers between devices, local(): lax.ppermute(even, 'gx', [(x, x ^ 1) for x in range(across) if x ^ 1 < ac...  0.74 us
  transfers between devices with their start and end apart: 5, of which 2 were waited for; matrix products, arithmetic and copies ran while one was open for 0% of the time, Pallas kernels for 0%

profile of v3, /device:TPU:17, one launch (start us, length us, event | category | flops | bytes accessed | tf_op | source)
XLA Modules:
  0.0 19.8 jit_solution(9154619382944091129)
XLA Ops:
  0.6 0.9 %pack_x.1 = (f32[64,256]{1,0:T(8,128)S(1)}, f32[64,256]{1,0:T(8,128)S(1)}) custom-call(f32[4,16,256]{2,1,0:T(8,128)} %potential_ref.5, f32[2,4,16,256]{3,2,1,0:T(8,128)} %angle_ref.5, f32[9,256]{1,0:T(8,128)} %deform_ref.3, s32[1,4,64]{2,1,0:T(4,128)} %slot_ref.3), custom_call_target="tpu_custom_call" | custom-call | tf_op jit(solution)/shard_map/pack_x/pallas_call | solution.py:544
  1.6 0.7 %collective-permute-start = (f32[64,256]{1,0:T(8,128)S(1)}, f32[64,256]{1,0:T(8,128)S(1)}, u32[]{:S(2)}, u32[]{:S(2)}) collective-permute-start(f32[64,256]{1,0:T(8,128)S(1)} %get-tuple-element.9), channel_id=1, source_target_pairs={{0,4},{4,0},{8,12},{12,8},{16,20},{20,16},{24,28},{28,24},{1,5},{5... | collective-permute-start | bytes 196616 | tf_op jit(solution)/shard_map/ppermute | solution.py:549
  2.3 3.1 %collective-permute-start.1 = (f32[64,256]{1,0:T(8,128)S(1)}, f32[64,256]{1,0:T(8,128)S(1)}, u32[]{:S(2)}, u32[]{:S(2)}) collective-permute-start(f32[64,256]{1,0:T(8,128)S(1)} %get-tuple-element.10), channel_id=1, source_target_pairs={{4,8},{12,16},{20,24},{8,4},{16,12},{24,20},{5,9},{13,17},{21,25},... | collective-permute-start | bytes 196616 | tf_op jit(solution)/shard_map/ppermute | solution.py:551
  5.4 0.0 collective-permute-done.even_ref
  5.4 2.5 %collective-permute-done.1.odd_ref = f32[64,256]{1,0:T(8,128)S(1)} collective-permute-done((f32[64,256]{1,0:T(8,128)S(1)}, f32[64,256]{1,0:T(8,128)S(1)}, u32[]{:S(2)}, u32[]{:S(2)}) %collective-permute-start.1) | collective-permute-done | bytes 65568 | tf_op jit(solution)/shard_map/ppermute | solution.py:551
  7.9 0.9 %pack_y.1 = (f32[48,256]{1,0:T(8,128)S(1)}, f32[48,256]{1,0:T(8,128)S(1)}, f32[48,256]{1,0:T(8,128)S(1)}, f32[64,256]{1,0:T(8,128)S(1)}, f32[64,256]{1,0:T(8,128)S(1)}) custom-call(f32[4,16,256]{2,1,0:T(8,128)} %potential_ref.5, f32[2,4,16,256]{3,2,1,0:T(8,128)} %angle_ref.5, f32[9,256]{1,0:T(8,128)} %deform_ref.3, s32[1,4,64]{2,1,0:T(4,128)} %slot_ref.3, ...), custom_call_target="tpu_custom_call" | custom-call | tf_op jit(solution)/shard_map/pack_y/pallas_call | solution.py:554
  8.8 1.3 %collective-permute-start.2 = (f32[64,256]{1,0:T(8,128)S(1)}, f32[64,256]{1,0:T(8,128)S(1)}, u32[]{:S(2)}, u32[]{:S(2)}) collective-permute-start(f32[64,256]{1,0:T(8,128)S(1)} %get-tuple-element.14), channel_id=1, source_target_pairs={{0,1},{1,0},{2,3},{3,2},{4,5},{5,4},{6,7},{7,6},{8,9},{9,8},{10,11... | collective-permute-start | bytes 196616 | tf_op jit(solution)/shard_map/ppermute | solution.py:565
  10.1 1.2 %collective-permute-start.4 = (f32[64,256]{1,0:T(8,128)S(1)}, f32[64,256]{1,0:T(8,128)S(1)}, u32[]{:S(2)}, u32[]{:S(2)}) collective-permute-start(f32[64,256]{1,0:T(8,128)S(1)} %get-tuple-element.15), channel_id=1, source_target_pairs={{0,3},{1,2},{2,1},{3,0},{4,7},{5,6},{6,5},{7,4},{8,11},{9,10},{10,... | collective-permute-start | bytes 196616 | tf_op jit(solution)/shard_map/ppermute | solution.py:565
  11.3 0.2 %collective-permute-start.3 = (f32[48,256]{1,0:T(8,128)S(1)}, f32[48,256]{1,0:T(8,128)S(1)}, u32[]{:S(2)}, u32[]{:S(2)}) collective-permute-start(f32[48,256]{1,0:T(8,128)S(1)} %get-tuple-element.13.refs_0_), channel_id=1, source_target_pairs={{0,2},{1,3},{2,0},{3,1},{4,6},{5,7},{6,4},{7,5},{8,10},{9,11},{10,... | collective-permute-start | bytes 147464 | tf_op jit(solution)/shard_map/ppermute | solution.py:565
  11.5 4.6 %collective-permute-done.3.refs_2_ = f32[48,256]{1,0:T(8,128)S(1)} collective-permute-done((f32[48,256]{1,0:T(8,128)S(1)}, f32[48,256]{1,0:T(8,128)S(1)}, u32[]{:S(2)}, u32[]{:S(2)}) %collective-permute-start.3) | collective-permute-done | bytes 49184 | tf_op jit(solution)/shard_map/ppermute | solution.py:565
  16.1 0.0 collective-permute-done.2.refs_1_
  16.1 0.0 collective-permute-done.4.refs_3_
  16.1 3.6 %step.1 = (f32[4,16,256]{2,1,0:T(8,128)}, f32[4,16,256]{2,1,0:T(8,128)}) custom-call(f32[4,16,256]{2,1,0:T(8,128)} %potential_ref.5, f32[4,16,256]{2,1,0:T(8,128)} %recovery_ref.1, f32[2,4,16,256]{3,2,1,0:T(8,128)} %angle_ref.5, f32[48,256]{1,0:T(8,128)S(1)} %get-tuple-element.11.low_ref, f32[48,256]{1,0:T(8,128)S(1)} %get-tuple-element.12.high_ref, ...), custom_call_target="tpu_custom_call" | custom-call | tf_op jit(solution)/shard_map/step/pallas_call | solution.py:568
Async XLA Ops:
  1.6 3.9 %collective-permute-start = (f32[64,256]{1,0:T(8,128)S(1)}, f32[64,256]{1,0:T(8,128)S(1)}, u32[]{:S(2)}, u32[]{:S(2)}) collective-permute-start(f32[64,256]{1,0:T(8,128)S(1)} %get-tuple-element.9), channel_id=1, source_target_pairs={{0,4},{4,0},{8,12},{12,8},{16,20},{20,16},{24,28},{28,24},{1,5},{5... | collective-permute-start | bytes 196616 | tf_op jit(solution)/shard_map/ppermute | solution.py:549
  2.3 5.6 %collective-permute-start.1 = (f32[64,256]{1,0:T(8,128)S(1)}, f32[64,256]{1,0:T(8,128)S(1)}, u32[]{:S(2)}, u32[]{:S(2)}) collective-permute-start(f32[64,256]{1,0:T(8,128)S(1)} %get-tuple-element.10), channel_id=1, source_target_pairs={{4,8},{12,16},{20,24},{8,4},{16,12},{24,20},{5,9},{13,17},{21,25},... | collective-permute-start | bytes 196616 | tf_op jit(solution)/shard_map/ppermute | solution.py:551
  8.8 7.3 %collective-permute-start.2 = (f32[64,256]{1,0:T(8,128)S(1)}, f32[64,256]{1,0:T(8,128)S(1)}, u32[]{:S(2)}, u32[]{:S(2)}) collective-permute-start(f32[64,256]{1,0:T(8,128)S(1)} %get-tuple-element.14), channel_id=1, source_target_pairs={{0,1},{1,0},{2,3},{3,2},{4,5},{5,4},{6,7},{7,6},{8,9},{9,8},{10,11... | collective-permute-start | bytes 196616 | tf_op jit(solution)/shard_map/ppermute | solution.py:565
  10.1 6.0 %collective-permute-start.4 = (f32[64,256]{1,0:T(8,128)S(1)}, f32[64,256]{1,0:T(8,128)S(1)}, u32[]{:S(2)}, u32[]{:S(2)}) collective-permute-start(f32[64,256]{1,0:T(8,128)S(1)} %get-tuple-element.15), channel_id=1, source_target_pairs={{0,3},{1,2},{2,1},{3,0},{4,7},{5,6},{6,5},{7,4},{8,11},{9,10},{10,... | collective-permute-start | bytes 196616 | tf_op jit(solution)/shard_map/ppermute | solution.py:565
  11.3 4.8 %collective-permute-start.3 = (f32[48,256]{1,0:T(8,128)S(1)}, f32[48,256]{1,0:T(8,128)S(1)}, u32[]{:S(2)}, u32[]{:S(2)}) collective-permute-start(f32[48,256]{1,0:T(8,128)S(1)} %get-tuple-element.13.refs_0_), channel_id=1, source_target_pairs={{0,2},{1,3},{2,0},{3,1},{4,6},{5,7},{6,4},{7,5},{8,10},{9,11},{10,... | collective-permute-start | bytes 147464 | tf_op jit(solution)/shard_map/ppermute | solution.py:565

commit v4 on v3

--- a/solution.py
+++ b/solution.py
@@ -91,45 +91,73 @@
     ].astype(jnp.float32)
 
 
-def pack_x(potential_ref, angle_ref, deform_ref, slot_ref, even_ref, odd_ref, *, rows):
+def pack_x(
+    potential_ref, angle_ref, deform_ref, slot_ref, even_ref, odd_ref, even_bulk, odd_bulk, *, rows
+):
     cells_x, cells_y = potential_ref.shape[:2]
+    corner = deform_ref.shape[0] + slot_ref.shape[1]
     gx = lax.axis_index("gx")
-    for out_ref, goes_up in ((even_ref, gx % 2 == 0), (odd_ref, gx % 2 == 1)):
+    for out_ref, bulk_ref, goes_up in (
+        (even_ref, even_bulk, gx % 2 == 0),
+        (odd_ref, odd_bulk, gx % 2 == 1),
+    ):
+        fill_gradients(out_ref, 0, deform_ref, slot_ref, rows)
         sources = (potential_ref, angle_ref.at[0], angle_ref.at[1])
         for number, source in enumerate(sources):
-            out_ref[number * cells_y : (number + 1) * cells_y] = jnp.where(
-                goes_up, source[cells_x - 1], source[0]
-            )
-        fill_gradients(out_ref, 3 * cells_y, deform_ref, slot_ref, rows)
+            edge = jnp.where(goes_up, source[cells_x - 1], source[0])
+            bulk_ref[number * cells_y : (number + 1) * cells_y] = edge
+            if number == 0:
+                out_ref[corner : corner + 1] = edge[0:1]
+                out_ref[corner + 1 : corner + 2] = edge[cells_y - 1 :]
 
 
 def pack_y(
     potential_ref, angle_ref, deform_ref, slot_ref, even_ref, odd_ref, *out_refs, rims, rows
 ):
-    low_ref, high_ref, row_ref = out_refs[:3]
+    row_ref, plain_ref = out_refs[:2]
     cells_x, cells_y, depth = potential_ref.shape
+    components = deform_ref.shape[0]
+    columns, coarse_depth = slot_ref.shape[1:]
+    corner = components + columns
     gx = lax.axis_index("gx")
     gy = lax.axis_index("gy")
-    at_first = gx == 0
-    at_last = gx == lax.axis_size("gx") - 1
     is_odd = gx % 2 == 1
     fill_gradients(row_ref, rows, deform_ref, slot_ref, rows)
-    even, odd = even_ref[3 * cells_y :], odd_ref[3 * cells_y :]
+    row_ref[rows + corner : rows + corner + 1] = potential_ref[0, 0:1]
+    row_ref[rows + corner + 1 : rows + corner + 2] = potential_ref[0, cells_y - 1 :]
     own = row_ref[rows : 2 * rows]
-    row_ref[0:rows] = jnp.where(at_first, own, jnp.where(is_odd, even, odd))
+    even, odd = even_ref[...], odd_ref[...]
+    row_ref[0:rows] = jnp.where(gx == 0, own, jnp.where(is_odd, even, odd))
+    row_ref[rows + corner : rows + corner + 1] = potential_ref[cells_x - 1, 0:1]
+    row_ref[rows + corner + 1 : rows + corner + 2] = potential_ref[cells_x - 1, cells_y - 1 :]
+    own = row_ref[rows : 2 * rows]
+    at_last = gx == lax.axis_size("gx") - 1
     row_ref[2 * rows :] = jnp.where(at_last, own, jnp.where(is_odd, odd, even))
-    for number, source in enumerate((potential_ref, angle_ref.at[0], angle_ref.at[1])):
-        part = slice(number * cells_y, (number + 1) * cells_y)
-        even, odd = even_ref[part], odd_ref[part]
-        low_ref[part] = jnp.where(at_first, source[0], jnp.where(is_odd, even, odd))
-        high_ref[part] = jnp.where(at_last, source[cells_x - 1], jnp.where(is_odd, odd, even))
+    plain_ref[3 * components :] = jnp.zeros(
+        (plain_ref.shape[0] - 3 * components, depth), jnp.float32
+    )
+    for r in range(3):
+        plain_ref[r * components : (r + 1) * components] = row_ref[r * rows : r * rows + components]
     first_rows = round_up(cells_x + 2, 8)
-    for flips, out_ref in zip(rims, out_refs[3:]):
+    for flips, out_ref in zip(rims, out_refs[2:]):
         goes_right = (gy ^ flips) > gy
-        start = out_ref.shape[0] - 3 * rows
-        out_ref[start:] = row_ref[...]
+        start = out_ref.shape[0] - plain_ref.shape[0]
+        out_ref[start:] = plain_ref[...]
         out_ref[0:start] = jnp.zeros((start, depth), jnp.float32)
-        lines = [(0, low_ref), (1 + cells_x, high_ref)]
+        for r in range(3):
+            first = r * rows + components
+            line = start + 3 * components + r
+            out_ref[line : line + 1] = jnp.where(
+                goes_right,
+                row_ref[first + columns - 1 : first + columns],
+                row_ref[first : first + 1],
+            )
+        for line, r in ((0, 0), (1 + cells_x, 2)):
+            first = r * rows + corner
+            out_ref[line : line + 1] = jnp.where(
+                goes_right, row_ref[first + 1 : first + 2], row_ref[first : first + 1]
+            )
+        lines = []
         for x in range(cells_x):
             lines.append((1 + x, potential_ref.at[x]))
             lines.append((first_rows + x, angle_ref.at[0, x]))
@@ -196,8 +224,8 @@
     potential_ref,
     recovery_ref,
     angle_ref,
-    low_ref,
-    high_ref,
+    even_ref,
+    odd_ref,
     line_ref,
     side_ref,
     deep_ref,
@@ -213,6 +241,8 @@
     (
         potential_out,
         recovery_out,
+        low_ref,
+        high_ref,
         coarse_ref,
         fine_ref,
         conduct_ref,
@@ -234,9 +264,25 @@
             chosen = jnp.where((gy ^ flips) == towards, value, chosen)
         return chosen
 
+    filler = jnp.zeros((rows - components, held), jnp.float32)
+    skip = round_up(cells_x + 2, 8) + 2 * cells_x
+
     def table(r, flips):
-        start = packets[flips].shape[0] - (elements + 2 - r) * rows
-        return packets[flips].at[start : start + rows]
+        if flips == 0:
+            return packets[0][r * rows : (r + 1) * rows]
+        start = r * components + (skip if is_rim(flips) else 0)
+        return jnp.concatenate([packets[flips][start : start + components], filler], axis=0)
+
+    def facing(r, flips):
+        start = skip + 3 * components + r
+        return packets[flips][start : start + 1, 0 : 2 * coarse_depth]
+
+    is_odd = gx % 2 == 1
+    for number, source in enumerate((potential_ref, angle_ref.at[0], angle_ref.at[1])):
+        part = slice(number * cells_y, (number + 1) * cells_y)
+        even, odd = even_ref[part], odd_ref[part]
+        low_ref[part] = jnp.where(at_first_x, source[0], jnp.where(is_odd, even, odd))
+        high_ref[part] = jnp.where(at_last_x, source[cells_x - 1], jnp.where(is_odd, odd, even))
 
     first_rows = round_up(cells_x + 2, 8)
     rim_rows = []
@@ -253,19 +299,14 @@
     count = columns + 2
     gathered = [[None] * (count // 2) for _ in range(elements + 2)]
     for r in range(elements + 2):
-        own = table(r, 0)[components : components + columns, 0:lanes]
-        last = components + columns - 1
-        before = beside(
-            {f: table(r, f)[last : last + 1, 0:lanes] for f in rims}, gy - 1, own[0:1]
-        )
-        after = beside(
-            {f: table(r, f)[components : components + 1, 0:lanes] for f in rims},
-            gy + 1,
-            own[columns - 1 : columns],
-        )
+        start = r * rows + components
+        own = packets[0][start : start + columns, 0:lanes]
+        values = {f: facing(r, f) for f in rims}
+        before = beside(values, gy - 1, own[0:1])
+        after = beside(values, gy + 1, own[columns - 1 : columns])
         line = [before] + [own[c : c + 1] for c in range(columns)] + [after]
         table_parts = parts_of(
-            jnp.concatenate([table(r, f)[:, 0:held] for f in range(devices)], axis=0), 3
+            jnp.concatenate([table(r, f) for f in range(devices)], axis=0), 3
         )
         for pair in range(count // 2):
             slots = jnp.where(
@@ -531,7 +572,7 @@
     cells_x, cells_y, depth = potential.shape
     elements, columns, coarse_depth = elem_slot.shape
     components, held = deform.shape
-    rows = round_up(components + columns + 1, 8)
+    rows = round_up(components + columns + 2, 8)
     weights = weights_of(cells_x, cells_y, columns, coarse_depth, depth, rows, components)
     across, down = lax.axis_size("gx"), lax.axis_size("gy")
     assert elements == 1 and columns % 2 == 0 and held == depth
@@ -541,28 +582,32 @@
         return OUT((count, depth))
 
     arrays = (potential, fiber_angles, deform, elem_slot)
-    even, odd = pl.pallas_call(
+    swaps = [[(x, x ^ 1) for x in range(across) if x ^ 1 < across]]
+    upward = [(x, x + 1) for x in range(1, across - 1, 2)]
+    swaps.append(upward + [(high, low) for low, high in upward])
+    even, odd, even_bulk, odd_bulk = pl.pallas_call(
         functools.partial(pack_x, rows=rows),
-        out_shape=[packet(3 * cells_y + rows)] * 2,
+        out_shape=[packet(rows)] * 2 + [packet(3 * cells_y)] * 2,
         name="pack_x",
     )(*arrays)
-    even = lax.ppermute(even, "gx", [(x, x ^ 1) for x in range(across) if x ^ 1 < across])
-    upward = [(x, x + 1) for x in range(1, across - 1, 2)]
-    odd = lax.ppermute(odd, "gx", upward + [(high, low) for low, high in upward])
+    odd = lax.ppermute(odd, "gx", swaps[1])
+    even = lax.ppermute(even, "gx", swaps[0])
+    odd_bulk = lax.ppermute(odd_bulk, "gx", swaps[1])
+    even_bulk = lax.ppermute(even_bulk, "gx", swaps[0])
     rims = [flips for flips in range(1, down) if is_rim(flips)]
     side_rows = round_up(cells_x + 2, 8) + 2 * cells_x
-    low, high, row, *sent = pl.pallas_call(
+    plain_rows = round_up(3 * components + 3, 8)
+    row, plain, *sent = pl.pallas_call(
         functools.partial(pack_y, rims=rims, rows=rows),
-        out_shape=[packet(3 * cells_y)] * 2
-        + [packet(3 * rows)]
-        + [packet(side_rows + 3 * rows)] * len(rims),
+        out_shape=[packet(3 * rows), packet(plain_rows)]
+        + [packet(side_rows + plain_rows)] * len(rims),
         name="pack_y",
-    )(*arrays, IN(even), IN(odd))
+    )(*[IN(value) for value in arrays], IN(even), IN(odd))
     sent = dict(zip(rims, sent))
     packets = [IN(row)]
     for flips in range(1, down):
         pairs = [(y, y ^ flips) for y in range(down)]
-        packets.append(IN(lax.ppermute(sent.get(flips, row), "gy", pairs)))
+        packets.append(IN(lax.ppermute(sent.get(flips, plain), "gy", pairs)))
     block = jax.ShapeDtypeStruct((cells_x, cells_y, depth), jnp.float32)
     line_count = (cells_x + 2) * cells_y + 2 * cells_x
     return pl.pallas_call(
@@ -577,13 +622,24 @@
         ),
         out_shape=(block, block),
         scratch_shapes=[
+            pltpu.VMEM((3 * cells_y, depth), jnp.float32),
+            pltpu.VMEM((3 * cells_y, depth), jnp.float32),
             pltpu.VMEM(((columns + 2) * (elements + 2) * rows, depth), jnp.float32),
             pltpu.VMEM((components * line_count, depth), jnp.float32),
             pltpu.VMEM((6, line_count, depth), jnp.float32),
             pltpu.VMEM((cells_x * cells_y, depth), jnp.float32),
         ],
         name="step",
-    )(potential, recovery, fiber_angles, IN(low), IN(high), *weights, *packets)
+    )(
+        IN(potential),
+        IN(recovery),
+        IN(fiber_angles),
+        IN(even_bulk),
+        IN(odd_bulk),
+        weights[0],
+        *[IN(value) for value in weights[1:]],
+        *packets,
+    )
 
 
 def solution(mesh):

time: 19.9 us -> 19.4 us (0.975)
  the two profiles are of different devices: /device:TPU:17 before, /device:TPU:1 now
where the time goes in v4:
time: 19.4 us; the launch traced here: 19.1 us
  starting transfers between devices  11.1 us (57%)
  Pallas kernels  4.34 us (22%)
  waiting for transfers between devices  2.77 us (14%)
  between operations  0.8 us (4%)
    ppermute x1, starting transfers between devices, local(): odd = lax.ppermute(odd, 'gx', swaps[1])  4.58 us
    ppermute x1, starting transfers between devices, local(): odd_bulk = lax.ppermute(odd_bulk, 'gx', swaps[1])  3.69 us
    pallas_call x1, Pallas kernels, local(): pl.pallas_call(functools.partial(step, components=components, held=held,...  3.32 us
    ppermute x3, waiting for transfers between devices, local(): packets.append(IN(lax.ppermute(sent.get(flips, plain), 'gy', pairs)))  2.76 us
    ppermute x3, starting transfers between devices, local(): packets.append(IN(lax.ppermute(sent.get(flips, plain), 'gy', pairs)))  2.71 us
    pallas_call x1, Pallas kernels, local(): pl.pallas_call(functools.partial(pack_x, rows=rows), out_shape=[packet(ro...  0.97 us
  transfers between devices with their start and end apart: 7, of which 1 were waited for; matrix products, arithmetic and copies ran while one was open for 0% of the time, Pallas kernels for 0%

profile of v4, /device:TPU:1, one launch (start us, length us, event | category | flops | bytes accessed | tf_op | source)
XLA Modules:
  0.0 19.1 jit_solution(4659231514421766108)
XLA Ops:
  0.6 0.0 copy-start
  0.6 0.0 copy-start.1
  0.6 0.0 copy-start.4
  0.7 1.0 %pack_x.1 = (f32[16,256]{1,0:T(8,128)S(1)}, f32[16,256]{1,0:T(8,128)S(1)}, f32[48,256]{1,0:T(8,128)S(1)}, f32[48,256]{1,0:T(8,128)S(1)}) custom-call(f32[4,16,256]{2,1,0:T(8,128)} %potential_ref.5, f32[2,4,16,256]{3,2,1,0:T(8,128)} %angle_ref.5, f32[9,256]{1,0:T(8,128)} %deform_ref.3, s32[1,4,64]{2,1,0:T(4,128)} %slot_ref.3), custom_call_target="tpu_custom_call" | custom-call | tf_op jit(solution)/shard_map/pack_x/pallas_call | solution.py:588
  1.6 0.0 copy-start.6
  1.6 0.0 copy-start.2
  1.7 0.1 collective-permute-start.2
  1.7 4.6 %collective-permute-start.3 = (f32[16,256]{1,0:T(8,128)S(1)}, f32[16,256]{1,0:T(8,128)S(1)}, u32[]{:S(2)}, u32[]{:S(2)}) collective-permute-start(f32[16,256]{1,0:T(8,128)S(1)} %get-tuple-element.13), channel_id=1, source_target_pairs={{4,8},{12,16},{20,24},{8,4},{16,12},{24,20},{5,9},{13,17},{21,25},... | collective-permute-start | bytes 49160 | tf_op jit(solution)/shard_map/ppermute | solution.py:593
  6.3 0.1 collective-permute-start
  6.4 0.0 copy-start.3
  6.4 0.0 copy-start.5
  6.4 3.7 %collective-permute-start.1 = (f32[48,256]{1,0:T(8,128)S(1)}, f32[48,256]{1,0:T(8,128)S(1)}, u32[]{:S(2)}, u32[]{:S(2)}) collective-permute-start(f32[48,256]{1,0:T(8,128)S(1)} %get-tuple-element.11), channel_id=1, source_target_pairs={{4,8},{12,16},{20,24},{8,4},{16,12},{24,20},{5,9},{13,17},{21,25},... | collective-permute-start | bytes 147464 | tf_op jit(solution)/shard_map/ppermute | solution.py:595
  10.1 0.0 collective-permute-done.2.even_ref
  10.1 0.0 collective-permute-done.3.odd_ref
  10.1 0.0 copy-done
  10.2 0.0 copy-done.1
  10.2 0.0 copy-done.4
  10.2 0.0 copy-done.6
  10.2 0.1 pack_y.1
  10.2 1.3 %collective-permute-start.4 = (f32[48,256]{1,0:T(8,128)S(1)}, f32[48,256]{1,0:T(8,128)S(1)}, u32[]{:S(2)}, u32[]{:S(2)}) collective-permute-start(f32[48,256]{1,0:T(8,128)S(1)} %get-tuple-element.15), channel_id=1, source_target_pairs={{0,1},{1,0},{2,3},{3,2},{4,5},{5,4},{6,7},{7,6},{8,9},{9,8},{10,11... | collective-permute-start | bytes 147464 | tf_op jit(solution)/shard_map/ppermute | solution.py:610
  11.5 1.2 %collective-permute-start.6 = (f32[48,256]{1,0:T(8,128)S(1)}, f32[48,256]{1,0:T(8,128)S(1)}, u32[]{:S(2)}, u32[]{:S(2)}) collective-permute-start(f32[48,256]{1,0:T(8,128)S(1)} %get-tuple-element.17), channel_id=1, source_target_pairs={{0,3},{1,2},{2,1},{3,0},{4,7},{5,6},{6,5},{7,4},{8,11},{9,10},{10,... | collective-permute-start | bytes 147464 | tf_op jit(solution)/shard_map/ppermute | solution.py:610
  12.7 0.2 %collective-permute-start.5 = (f32[32,256]{1,0:T(8,128)S(1)}, f32[32,256]{1,0:T(8,128)S(1)}, u32[]{:S(2)}, u32[]{:S(2)}) collective-permute-start(f32[32,256]{1,0:T(8,128)S(1)} %get-tuple-element.16), channel_id=1, source_target_pairs={{0,2},{1,3},{2,0},{3,1},{4,6},{5,7},{6,4},{7,5},{8,10},{9,11},{10,... | collective-permute-start | bytes 98312 | tf_op jit(solution)/shard_map/ppermute | solution.py:610
  13.0 2.8 %collective-permute-done.5.refs_2_ = f32[32,256]{1,0:T(8,128)S(1)} collective-permute-done((f32[32,256]{1,0:T(8,128)S(1)}, f32[32,256]{1,0:T(8,128)S(1)}, u32[]{:S(2)}, u32[]{:S(2)}) %collective-permute-start.5) | collective-permute-done | bytes 32800 | tf_op jit(solution)/shard_map/ppermute | solution.py:610
  15.7 0.0 collective-permute-done.even_ref
  15.7 0.0 collective-permute-done.1.odd_ref
  15.7 0.0 collective-permute-done.4.refs_1_
  15.7 0.0 collective-permute-done.6.refs_3_
  15.7 0.0 copy-done.2
  15.7 0.0 copy-done.3
  15.8 0.0 copy-done.5
  15.8 3.3 %step.1 = (f32[4,16,256]{2,1,0:T(8,128)}, f32[4,16,256]{2,1,0:T(8,128)}) custom-call(f32[4,16,256]{2,1,0:T(8,128)S(1)} %copy-done.1, f32[4,16,256]{2,1,0:T(8,128)S(1)} %copy-done.3, f32[2,4,16,256]{3,2,1,0:T(8,128)S(1)} %copy-done, f32[48,256]{1,0:T(8,128)S(1)} %collective-permute-done.even_ref, f32[48,256]{1,0:T(8,128)S(1)} %collective-permute-done.1.odd_ref, ...), custom_call_target="tpu_custom_call" | custom-call | tf_op jit(solution)/shard_map/step/pallas_call | solution.py:613
Async XLA Ops:
  0.6 9.5 %copy-start = (f32[2,4,16,256]{3,2,1,0:T(8,128)S(1)}, f32[2,4,16,256]{3,2,1,0:T(8,128)}, u32[]{:S(2)}) copy-start(f32[2,4,16,256]{3,2,1,0:T(8,128)} %angle_ref.5) | copy-start | bytes 393220
  0.6 9.5 %copy-start.1 = (f32[4,16,256]{2,1,0:T(8,128)S(1)}, f32[4,16,256]{2,1,0:T(8,128)}, u32[]{:S(2)}) copy-start(f32[4,16,256]{2,1,0:T(8,128)} %potential_ref.5) | copy-start | bytes 196612
  0.6 9.5 %copy-start.4 = (f32[9,256]{1,0:T(8,128)S(1)}, f32[9,256]{1,0:T(8,128)}, u32[]{:S(2)}) copy-start(f32[9,256]{1,0:T(8,128)} %deform_ref.3) | copy-start | bytes 27652
  1.6 8.5 %copy-start.6 = (s32[1,4,64]{2,1,0:T(4,128)S(1)}, s32[1,4,64]{2,1,0:T(4,128)}, u32[]{:S(2)}) copy-start(s32[1,4,64]{2,1,0:T(4,128)} %slot_ref.3) | copy-start | bytes 3076
  1.6 14.1 %copy-start.2 = (bf16[128,512]{1,0:T(8,128)(2,1)S(1)}, bf16[128,512]{1,0:T(8,128)(2,1)}, u32[]{:S(2)}) copy-start(bf16[128,512]{1,0:T(8,128)(2,1)} %constant.8.clone.deep_ref) | copy-start | bytes 393220
  1.7 8.5 %collective-permute-start.2 = (f32[16,256]{1,0:T(8,128)S(1)}, f32[16,256]{1,0:T(8,128)S(1)}, u32[]{:S(2)}, u32[]{:S(2)}) collective-permute-start(f32[16,256]{1,0:T(8,128)S(1)} %get-tuple-element.12), channel_id=1, source_target_pairs={{0,4},{4,0},{8,12},{12,8},{16,20},{20,16},{24,28},{28,24},{1,5},{5... | collective-permute-start | bytes 49160 | tf_op jit(solution)/shard_map/ppermute | solution.py:594
  1.7 8.4 %collective-permute-start.3 = (f32[16,256]{1,0:T(8,128)S(1)}, f32[16,256]{1,0:T(8,128)S(1)}, u32[]{:S(2)}, u32[]{:S(2)}) collective-permute-start(f32[16,256]{1,0:T(8,128)S(1)} %get-tuple-element.13), channel_id=1, source_target_pairs={{4,8},{12,16},{20,24},{8,4},{16,12},{24,20},{5,9},{13,17},{21,25},... | collective-permute-start | bytes 49160 | tf_op jit(solution)/shard_map/ppermute | solution.py:593
  6.3 9.4 %collective-permute-start = (f32[48,256]{1,0:T(8,128)S(1)}, f32[48,256]{1,0:T(8,128)S(1)}, u32[]{:S(2)}, u32[]{:S(2)}) collective-permute-start(f32[48,256]{1,0:T(8,128)S(1)} %get-tuple-element.10), channel_id=1, source_target_pairs={{0,4},{4,0},{8,12},{12,8},{16,20},{20,16},{24,28},{28,24},{1,5},{5... | collective-permute-start | bytes 147464 | tf_op jit(solution)/shard_map/ppermute | solution.py:596
  6.4 9.3 %copy-start.3 = (f32[4,16,256]{2,1,0:T(8,128)S(1)}, f32[4,16,256]{2,1,0:T(8,128)}, u32[]{:S(2)}) copy-start(f32[4,16,256]{2,1,0:T(8,128)} %recovery_ref.1) | copy-start | bytes 196612
  6.4 9.3 %copy-start.5 = (bf16[72,384]{1,0:T(8,128)(2,1)S(1)}, bf16[72,384]{1,0:T(8,128)(2,1)}, u32[]{:S(2)}) copy-start(bf16[72,384]{1,0:T(8,128)(2,1)} %constant.7.clone.side_ref) | copy-start | bytes 165892
  6.4 9.3 %collective-permute-start.1 = (f32[48,256]{1,0:T(8,128)S(1)}, f32[48,256]{1,0:T(8,128)S(1)}, u32[]{:S(2)}, u32[]{:S(2)}) collective-permute-start(f32[48,256]{1,0:T(8,128)S(1)} %get-tuple-element.11), channel_id=1, source_target_pairs={{4,8},{12,16},{20,24},{8,4},{16,12},{24,20},{5,9},{13,17},{21,25},... | collective-permute-start | bytes 147464 | tf_op jit(solution)/shard_map/ppermute | solution.py:595
  10.2 5.5 %collective-permute-start.4 = (f32[48,256]{1,0:T(8,128)S(1)}, f32[48,256]{1,0:T(8,128)S(1)}, u32[]{:S(2)}, u32[]{:S(2)}) collective-permute-start(f32[48,256]{1,0:T(8,128)S(1)} %get-tuple-element.15), channel_id=1, source_target_pairs={{0,1},{1,0},{2,3},{3,2},{4,5},{5,4},{6,7},{7,6},{8,9},{9,8},{10,11... | collective-permute-start | bytes 147464 | tf_op jit(solution)/shard_map/ppermute | solution.py:610
  11.5 4.2 %collective-permute-start.6 = (f32[48,256]{1,0:T(8,128)S(1)}, f32[48,256]{1,0:T(8,128)S(1)}, u32[]{:S(2)}, u32[]{:S(2)}) collective-permute-start(f32[48,256]{1,0:T(8,128)S(1)} %get-tuple-element.17), channel_id=1, source_target_pairs={{0,3},{1,2},{2,1},{3,0},{4,7},{5,6},{6,5},{7,4},{8,11},{9,10},{10,... | collective-permute-start | bytes 147464 | tf_op jit(solution)/shard_map/ppermute | solution.py:610
  12.7 3.0 %collective-permute-start.5 = (f32[32,256]{1,0:T(8,128)S(1)}, f32[32,256]{1,0:T(8,128)S(1)}, u32[]{:S(2)}, u32[]{:S(2)}) collective-permute-start(f32[32,256]{1,0:T(8,128)S(1)} %get-tuple-element.16), channel_id=1, source_target_pairs={{0,2},{1,3},{2,0},{3,1},{4,6},{5,7},{6,4},{7,5},{8,10},{9,11},{10,... | collective-permute-start | bytes 98312 | tf_op jit(solution)/shard_map/ppermute | solution.py:610

commit v5 on v4

--- a/solution.py
+++ b/solution.py
@@ -91,30 +91,22 @@
     ].astype(jnp.float32)
 
 
-def pack_x(
-    potential_ref, angle_ref, deform_ref, slot_ref, even_ref, odd_ref, even_bulk, odd_bulk, *, rows
-):
+def pack_x(potential_ref, deform_ref, slot_ref, even_ref, odd_ref, *, rows):
     cells_x, cells_y = potential_ref.shape[:2]
     corner = deform_ref.shape[0] + slot_ref.shape[1]
     gx = lax.axis_index("gx")
-    for out_ref, bulk_ref, goes_up in (
-        (even_ref, even_bulk, gx % 2 == 0),
-        (odd_ref, odd_bulk, gx % 2 == 1),
-    ):
+    for out_ref, goes_up in ((even_ref, gx % 2 == 0), (odd_ref, gx % 2 == 1)):
         fill_gradients(out_ref, 0, deform_ref, slot_ref, rows)
-        sources = (potential_ref, angle_ref.at[0], angle_ref.at[1])
-        for number, source in enumerate(sources):
-            edge = jnp.where(goes_up, source[cells_x - 1], source[0])
-            bulk_ref[number * cells_y : (number + 1) * cells_y] = edge
-            if number == 0:
-                out_ref[corner : corner + 1] = edge[0:1]
-                out_ref[corner + 1 : corner + 2] = edge[cells_y - 1 :]
+        for line, y in ((corner, 0), (corner + 1, cells_y - 1)):
+            out_ref[line : line + 1] = jnp.where(
+                goes_up, potential_ref[cells_x - 1, y : y + 1], potential_ref[0, y : y + 1]
+            )
 
 
 def pack_y(
     potential_ref, angle_ref, deform_ref, slot_ref, even_ref, odd_ref, *out_refs, rims, rows
 ):
-    row_ref, plain_ref = out_refs[:2]
+    row_ref, plain_ref, even_bulk, odd_bulk = out_refs[:4]
     cells_x, cells_y, depth = potential_ref.shape
     components = deform_ref.shape[0]
     columns, coarse_depth = slot_ref.shape[1:]
@@ -122,6 +114,11 @@
     gx = lax.axis_index("gx")
     gy = lax.axis_index("gy")
     is_odd = gx % 2 == 1
+    for bulk_ref, goes_up in ((even_bulk, gx % 2 == 0), (odd_bulk, gx % 2 == 1)):
+        for number, source in enumerate((potential_ref, angle_ref.at[0], angle_ref.at[1])):
+            bulk_ref[number * cells_y : (number + 1) * cells_y] = jnp.where(
+                goes_up, source[cells_x - 1], source[0]
+            )
     fill_gradients(row_ref, rows, deform_ref, slot_ref, rows)
     row_ref[rows + corner : rows + corner + 1] = potential_ref[0, 0:1]
     row_ref[rows + corner + 1 : rows + corner + 2] = potential_ref[0, cells_y - 1 :]
@@ -139,7 +136,7 @@
     for r in range(3):
         plain_ref[r * components : (r + 1) * components] = row_ref[r * rows : r * rows + components]
     first_rows = round_up(cells_x + 2, 8)
-    for flips, out_ref in zip(rims, out_refs[2:]):
+    for flips, out_ref in zip(rims, out_refs[4:]):
         goes_right = (gy ^ flips) > gy
         start = out_ref.shape[0] - plain_ref.shape[0]
         out_ref[start:] = plain_ref[...]
@@ -585,21 +582,20 @@
     swaps = [[(x, x ^ 1) for x in range(across) if x ^ 1 < across]]
     upward = [(x, x + 1) for x in range(1, across - 1, 2)]
     swaps.append(upward + [(high, low) for low, high in upward])
-    even, odd, even_bulk, odd_bulk = pl.pallas_call(
+    even, odd = pl.pallas_call(
         functools.partial(pack_x, rows=rows),
-        out_shape=[packet(rows)] * 2 + [packet(3 * cells_y)] * 2,
+        out_shape=[packet(rows)] * 2,
         name="pack_x",
-    )(*arrays)
+    )(potential, deform, elem_slot)
     odd = lax.ppermute(odd, "gx", swaps[1])
     even = lax.ppermute(even, "gx", swaps[0])
-    odd_bulk = lax.ppermute(odd_bulk, "gx", swaps[1])
-    even_bulk = lax.ppermute(even_bulk, "gx", swaps[0])
     rims = [flips for flips in range(1, down) if is_rim(flips)]
     side_rows = round_up(cells_x + 2, 8) + 2 * cells_x
     plain_rows = round_up(3 * components + 3, 8)
-    row, plain, *sent = pl.pallas_call(
+    row, plain, even_bulk, odd_bulk, *sent = pl.pallas_call(
         functools.partial(pack_y, rims=rims, rows=rows),
         out_shape=[packet(3 * rows), packet(plain_rows)]
+        + [packet(3 * cells_y)] * 2
         + [packet(side_rows + plain_rows)] * len(rims),
         name="pack_y",
     )(*[IN(value) for value in arrays], IN(even), IN(odd))
@@ -608,6 +604,8 @@
     for flips in range(1, down):
         pairs = [(y, y ^ flips) for y in range(down)]
         packets.append(IN(lax.ppermute(sent.get(flips, plain), "gy", pairs)))
+    odd_bulk = lax.ppermute(odd_bulk, "gx", swaps[1])
+    even_bulk = lax.ppermute(even_bulk, "gx", swaps[0])
     block = jax.ShapeDtypeStruct((cells_x, cells_y, depth), jnp.float32)
     line_count = (cells_x + 2) * cells_y + 2 * cells_x
     return pl.pallas_call(

time: 19.4 us -> 22.9 us (1.18)
  local copies, waits for them, and re-layouts: 0.04 us -> 1.83 us
  waiting for transfers between devices: 2.77 us -> 4.16 us
  starting transfers between devices: 11.1 us -> 11.5 us
    unnamed x14 -> x16, local copies, waits for them, and re-layouts: 0.04 us -> 1.83 us
    ppermute x1, waiting for transfers between devices: 0.01 us -> 1.4 us  [local(): odd = lax.ppermute(odd, 'gx', swaps[1])]
    ppermute x1, starting transfers between devices: 3.69 us -> 4.1 us  [local(): odd_bulk = lax.ppermute(odd_bulk, 'gx', swaps[1])]
  transfers between devices with their start and end apart: 7 -> 7, of which waited for: 1 -> 2; matrix products, arithmetic and copies ran while one was open for 0% -> 0% of each run, Pallas kernels for 0% -> 0%
where the time goes in v5:
time: 22.9 us; the launch traced here: 22.6 us
  starting transfers between devices  11.5 us (50%)
  Pallas kernels  4.29 us (19%)
  waiting for transfers between devices  4.16 us (18%)
  local copies, waits for them, and re-layouts  1.83 us (8%)
  between operations  0.75 us (3%)
    ppermute x1, starting transfers between devices, local(): odd = lax.ppermute(odd, 'gx', swaps[1])  4.58 us
    ppermute x1, starting transfers between devices, local(): odd_bulk = lax.ppermute(odd_bulk, 'gx', swaps[1])  4.1 us
    pallas_call x1, Pallas kernels, local(): pl.pallas_call(functools.partial(step, components=components, held=held,...  3.34 us
    ppermute x3, waiting for transfers between devices, local(): packets.append(IN(lax.ppermute(sent.get(flips, plain), 'gy', pairs)))  2.76 us
    ppermute x3, starting transfers between devices, local(): packets.append(IN(lax.ppermute(sent.get(flips, plain), 'gy', pairs)))  2.71 us
    unnamed x16, local copies, waits for them, and re-layouts  1.83 us
    ppermute x1, waiting for transfers between devices, local(): odd = lax.ppermute(odd, 'gx', swaps[1])  1.4 us
    pallas_call x1, Pallas kernels, local(): pl.pallas_call(functools.partial(pack_x, rows=rows), out_shape=[packet(ro...  0.9 us
  transfers between devices with their start and end apart: 7, of which 2 were waited for; matrix products, arithmetic and copies ran while one was open for 0% of the time, Pallas kernels for 0%

profile of v5, /device:TPU:1, one launch (start us, length us, event | category | flops | bytes accessed | tf_op | source)
XLA Modules:
  0.0 22.6 jit_solution(4921512463826803523)
XLA Ops:
  0.6 0.0 copy-start
  0.6 0.0 copy-start.5
  0.6 0.9 %pack_x.1 = (f32[16,256]{1,0:T(8,128)S(1)}, f32[16,256]{1,0:T(8,128)S(1)}) custom-call(f32[4,16,256]{2,1,0:T(8,128)} %potential_ref.5, f32[9,256]{1,0:T(8,128)} %deform_ref.3, s32[1,4,64]{2,1,0:T(4,128)} %slot_ref.3), custom_call_target="tpu_custom_call" | custom-call | tf_op jit(solution)/shard_map/pack_x/pallas_call | solution.py:585
  1.6 0.0 copy-start.7
  1.6 0.1 collective-permute-start
  1.7 4.6 %collective-permute-start.1 = (f32[16,256]{1,0:T(8,128)S(1)}, f32[16,256]{1,0:T(8,128)S(1)}, u32[]{:S(2)}, u32[]{:S(2)}) collective-permute-start(f32[16,256]{1,0:T(8,128)S(1)} %get-tuple-element.11), channel_id=1, source_target_pairs={{4,8},{12,16},{20,24},{8,4},{16,12},{24,20},{5,9},{13,17},{21,25},... | collective-permute-start | bytes 49160 | tf_op jit(solution)/shard_map/ppermute | solution.py:590
  6.2 0.0 collective-permute-done.even_ref
  6.2 1.4 %collective-permute-done.1.odd_ref = f32[16,256]{1,0:T(8,128)S(1)} collective-permute-done((f32[16,256]{1,0:T(8,128)S(1)}, f32[16,256]{1,0:T(8,128)S(1)}, u32[]{:S(2)}, u32[]{:S(2)}) %collective-permute-start.1) | collective-permute-done | bytes 16416 | tf_op jit(solution)/shard_map/ppermute | solution.py:590
  7.6 0.0 copy-done
  7.7 0.0 copy-done.5
  7.7 0.0 copy-done.7
  7.7 0.0 copy-start.1
  7.7 0.9 %copy-done.1 = f32[2,4,16,256]{3,2,1,0:T(8,128)S(1)} copy-done((f32[2,4,16,256]{3,2,1,0:T(8,128)S(1)}, f32[2,4,16,256]{3,2,1,0:T(8,128)}, u32[]{:S(2)}) %copy-start.1) | copy-done | bytes 131096
  8.6 0.0 copy-start.2
  8.6 0.0 copy-start.4
  8.6 0.0 copy-start.6
  8.6 0.1 pack_y.1
  8.6 0.1 collective-permute-start.2
  8.7 4.1 %collective-permute-start.3 = (f32[48,256]{1,0:T(8,128)S(1)}, f32[48,256]{1,0:T(8,128)S(1)}, u32[]{:S(2)}, u32[]{:S(2)}) collective-permute-start(f32[48,256]{1,0:T(8,128)S(1)} %get-tuple-element.13), channel_id=1, source_target_pairs={{4,8},{12,16},{20,24},{8,4},{16,12},{24,20},{5,9},{13,17},{21,25},... | collective-permute-start | bytes 147464 | tf_op jit(solution)/shard_map/ppermute | solution.py:607
  12.8 1.3 %collective-permute-start.4 = (f32[48,256]{1,0:T(8,128)S(1)}, f32[48,256]{1,0:T(8,128)S(1)}, u32[]{:S(2)}, u32[]{:S(2)}) collective-permute-start(f32[48,256]{1,0:T(8,128)S(1)} %get-tuple-element.15), channel_id=1, source_target_pairs={{0,1},{1,0},{2,3},{3,2},{4,5},{5,4},{6,7},{7,6},{8,9},{9,8},{10,11... | collective-permute-start | bytes 147464 | tf_op jit(solution)/shard_map/ppermute | solution.py:606
  14.1 1.2 %collective-permute-start.6 = (f32[48,256]{1,0:T(8,128)S(1)}, f32[48,256]{1,0:T(8,128)S(1)}, u32[]{:S(2)}, u32[]{:S(2)}) collective-permute-start(f32[48,256]{1,0:T(8,128)S(1)} %get-tuple-element.17), channel_id=1, source_target_pairs={{0,3},{1,2},{2,1},{3,0},{4,7},{5,6},{6,5},{7,4},{8,11},{9,10},{10,... | collective-permute-start | bytes 147464 | tf_op jit(solution)/shard_map/ppermute | solution.py:606
  15.3 0.2 %collective-permute-start.5 = (f32[32,256]{1,0:T(8,128)S(1)}, f32[32,256]{1,0:T(8,128)S(1)}, u32[]{:S(2)}, u32[]{:S(2)}) collective-permute-start(f32[32,256]{1,0:T(8,128)S(1)} %get-tuple-element.16), channel_id=1, source_target_pairs={{0,2},{1,3},{2,0},{3,1},{4,6},{5,7},{6,4},{7,5},{8,10},{9,11},{10,... | collective-permute-start | bytes 98312 | tf_op jit(solution)/shard_map/ppermute | solution.py:606
  15.5 2.8 %collective-permute-done.5.refs_2_ = f32[32,256]{1,0:T(8,128)S(1)} collective-permute-done((f32[32,256]{1,0:T(8,128)S(1)}, f32[32,256]{1,0:T(8,128)S(1)}, u32[]{:S(2)}, u32[]{:S(2)}) %collective-permute-start.5) | collective-permute-done | bytes 32800 | tf_op jit(solution)/shard_map/ppermute | solution.py:606
  18.3 0.0 collective-permute-done.2.even_ref
  18.3 0.0 collective-permute-done.3.odd_ref
  18.3 0.0 collective-permute-done.4.refs_1_
  18.3 0.0 collective-permute-done.6.refs_3_
  18.3 0.0 copy-done.2
  18.3 0.0 copy-done.4
  18.3 0.0 copy-done.6
  18.3 0.0 copy-start.3
  18.3 0.9 %copy-done.3 = bf16[128,512]{1,0:T(8,128)(2,1)S(1)} copy-done((bf16[128,512]{1,0:T(8,128)(2,1)S(1)}, bf16[128,512]{1,0:T(8,128)(2,1)}, u32[]{:S(2)}) %copy-start.3) | copy-done | bytes 131096
  19.2 3.3 %step.1 = (f32[4,16,256]{2,1,0:T(8,128)}, f32[4,16,256]{2,1,0:T(8,128)}) custom-call(f32[4,16,256]{2,1,0:T(8,128)S(1)} %copy-done, f32[4,16,256]{2,1,0:T(8,128)S(1)} %copy-done.4, f32[2,4,16,256]{3,2,1,0:T(8,128)S(1)} %copy-done.2, f32[48,256]{1,0:T(8,128)S(1)} %collective-permute-done.2.even_ref, f32[48,256]{1,0:T(8,128)S(1)} %collective-permute-done.3.odd_ref, ...), custom_call_target="tpu_custom_call" | custom-call | tf_op jit(solution)/shard_map/step/pallas_call | solution.py:611
Async XLA Ops:
  0.6 7.0 %copy-start = (f32[4,16,256]{2,1,0:T(8,128)S(1)}, f32[4,16,256]{2,1,0:T(8,128)}, u32[]{:S(2)}) copy-start(f32[4,16,256]{2,1,0:T(8,128)} %potential_ref.5) | copy-start | bytes 196612
  0.6 7.0 %copy-start.5 = (f32[9,256]{1,0:T(8,128)S(1)}, f32[9,256]{1,0:T(8,128)}, u32[]{:S(2)}) copy-start(f32[9,256]{1,0:T(8,128)} %deform_ref.3) | copy-start | bytes 27652
  1.6 6.1 %copy-start.7 = (s32[1,4,64]{2,1,0:T(4,128)S(1)}, s32[1,4,64]{2,1,0:T(4,128)}, u32[]{:S(2)}) copy-start(s32[1,4,64]{2,1,0:T(4,128)} %slot_ref.3) | copy-start | bytes 3076
  1.6 4.7 %collective-permute-start = (f32[16,256]{1,0:T(8,128)S(1)}, f32[16,256]{1,0:T(8,128)S(1)}, u32[]{:S(2)}, u32[]{:S(2)}) collective-permute-start(f32[16,256]{1,0:T(8,128)S(1)} %get-tuple-element.10), channel_id=1, source_target_pairs={{0,4},{4,0},{8,12},{12,8},{16,20},{20,16},{24,28},{28,24},{1,5},{5... | collective-permute-start | bytes 49160 | tf_op jit(solution)/shard_map/ppermute | solution.py:591
  1.7 6.0 %collective-permute-start.1 = (f32[16,256]{1,0:T(8,128)S(1)}, f32[16,256]{1,0:T(8,128)S(1)}, u32[]{:S(2)}, u32[]{:S(2)}) collective-permute-start(f32[16,256]{1,0:T(8,128)S(1)} %get-tuple-element.11), channel_id=1, source_target_pairs={{4,8},{12,16},{20,24},{8,4},{16,12},{24,20},{5,9},{13,17},{21,25},... | collective-permute-start | bytes 49160 | tf_op jit(solution)/shard_map/ppermute | solution.py:590
  7.7 0.9 %copy-start.1 = (f32[2,4,16,256]{3,2,1,0:T(8,128)S(1)}, f32[2,4,16,256]{3,2,1,0:T(8,128)}, u32[]{:S(2)}) copy-start(f32[2,4,16,256]{3,2,1,0:T(8,128)} %angle_ref.3) | copy-start | bytes 393220
  8.6 9.7 %copy-start.2 = (f32[2,4,16,256]{3,2,1,0:T(8,128)S(1)}, f32[2,4,16,256]{3,2,1,0:T(8,128)}, u32[]{:S(2)}) copy-start(f32[2,4,16,256]{3,2,1,0:T(8,128)} %angle_ref.3) | copy-start | bytes 393220
  8.6 9.7 %copy-start.4 = (f32[4,16,256]{2,1,0:T(8,128)S(1)}, f32[4,16,256]{2,1,0:T(8,128)}, u32[]{:S(2)}) copy-start(f32[4,16,256]{2,1,0:T(8,128)} %recovery_ref.1) | copy-start | bytes 196612
  8.6 9.8 %copy-start.6 = (bf16[72,384]{1,0:T(8,128)(2,1)S(1)}, bf16[72,384]{1,0:T(8,128)(2,1)}, u32[]{:S(2)}) copy-start(bf16[72,384]{1,0:T(8,128)(2,1)} %constant.7.clone.side_ref) | copy-start | bytes 165892
  8.6 9.7 %collective-permute-start.2 = (f32[48,256]{1,0:T(8,128)S(1)}, f32[48,256]{1,0:T(8,128)S(1)}, u32[]{:S(2)}, u32[]{:S(2)}) collective-permute-start(f32[48,256]{1,0:T(8,128)S(1)} %get-tuple-element.12), channel_id=1, source_target_pairs={{0,4},{4,0},{8,12},{12,8},{16,20},{20,16},{24,28},{28,24},{1,5},{5... | collective-permute-start | bytes 147464 | tf_op jit(solution)/shard_map/ppermute | solution.py:608
  8.7 9.6 %collective-permute-start.3 = (f32[48,256]{1,0:T(8,128)S(1)}, f32[48,256]{1,0:T(8,128)S(1)}, u32[]{:S(2)}, u32[]{:S(2)}) collective-permute-start(f32[48,256]{1,0:T(8,128)S(1)} %get-tuple-element.13), channel_id=1, source_target_pairs={{4,8},{12,16},{20,24},{8,4},{16,12},{24,20},{5,9},{13,17},{21,25},... | collective-permute-start | bytes 147464 | tf_op jit(solution)/shard_map/ppermute | solution.py:607
  12.8 5.5 %collective-permute-start.4 = (f32[48,256]{1,0:T(8,128)S(1)}, f32[48,256]{1,0:T(8,128)S(1)}, u32[]{:S(2)}, u32[]{:S(2)}) collective-permute-start(f32[48,256]{1,0:T(8,128)S(1)} %get-tuple-element.15), channel_id=1, source_target_pairs={{0,1},{1,0},{2,3},{3,2},{4,5},{5,4},{6,7},{7,6},{8,9},{9,8},{10,11... | collective-permute-start | bytes 147464 | tf_op jit(solution)/shard_map/ppermute | solution.py:606
  14.1 4.2 %collective-permute-start.6 = (f32[48,256]{1,0:T(8,128)S(1)}, f32[48,256]{1,0:T(8,128)S(1)}, u32[]{:S(2)}, u32[]{:S(2)}) collective-permute-start(f32[48,256]{1,0:T(8,128)S(1)} %get-tuple-element.17), channel_id=1, source_target_pairs={{0,3},{1,2},{2,1},{3,0},{4,7},{5,6},{6,5},{7,4},{8,11},{9,10},{10,... | collective-permute-start | bytes 147464 | tf_op jit(solution)/shard_map/ppermute | solution.py:606
  15.3 3.0 %collective-permute-start.5 = (f32[32,256]{1,0:T(8,128)S(1)}, f32[32,256]{1,0:T(8,128)S(1)}, u32[]{:S(2)}, u32[]{:S(2)}) collective-permute-start(f32[32,256]{1,0:T(8,128)S(1)} %get-tuple-element.16), channel_id=1, source_target_pairs={{0,2},{1,3},{2,0},{3,1},{4,6},{5,7},{6,4},{7,5},{8,10},{9,11},{10,... | collective-permute-start | bytes 98312 | tf_op jit(solution)/shard_map/ppermute | solution.py:606
  18.3 0.9 %copy-start.3 = (bf16[128,512]{1,0:T(8,128)(2,1)S(1)}, bf16[128,512]{1,0:T(8,128)(2,1)}, u32[]{:S(2)}) copy-start(bf16[128,512]{1,0:T(8,128)(2,1)} %constant.8.clone.deep_ref) | copy-start | bytes 393220
